TPU v7x, 1024 devices: a whole 4x8x16 slice. The times are simulated.
1024 devices in a mesh: dp: 16 (over y, core), expert: 64 (over z, x).
Axes of the slice: x: 4, y: 8, z: 16, core: 2. Of those that a mesh axis runs over, the one named last changes fastest.
Arguments:
- tokens: bfloat16 [131072, 1024], P(('dp', 'expert')), may hold values from -6 to 6
- cotangent: bfloat16 [131072, 1024], P(('dp', 'expert')), may hold values from -0.1875 to 0.1875
- expert_ids: int32 [131072, 4], P(('dp', 'expert')), may hold values from 0 to 63, all different within a row; in each aligned block of 128 rows (0 to 127, 128 to 255, ...) at most 16 rows name the same one
- gate_probs: bfloat16 [131072, 4], P(('dp', 'expert')), may hold values from 0.019897461 to 0.59765625
- home_share: int32 [32], replicated, may hold values from 4 to 8
- gate_weight: bfloat16 [64, 1024, 384], P('expert'), may hold values from -0.1875 to 0.1875
- up_weight: bfloat16 [64, 1024, 384], P('expert'), may hold values from -0.1875 to 0.1875
- down_weight: bfloat16 [64, 384, 1024], P('expert'), may hold values from -0.3125 to 0.3125
Outputs:
- gate_cotangent: float32 [131072, 4], P(('dp', 'expert'))
- grad_gate: float32 [64, 1024, 384], P('expert', 'dp')
- grad_up: float32 [64, 1024, 384], P('expert', 'dp')
- grad_down: float32 [64, 384, 1024], P('expert', 'dp')
Inputs may be any that keep to these rules, and one draw needn't show every extreme that they name: `expert_ids`: each token names 4 different experts; among the tokens of one device no expert is named more than 16 times.
All inputs are finite; a program needn't handle non-finite values.
Results may differ from a plain program's by a relative error of at most 0.017.
Values may be sent and summed in bfloat16 or wider, within the bound.
A program may use at most 64 MiB of HBM per device.

v0:
```python
import jax
import jax.numpy as jnp
from jax import lax
from jax.sharding import PartitionSpec as P


def in_one_piece(arrays, axis, split_dim, concat_dim, along):
    columns = [a.reshape(*a.shape[:along], -1) for a in arrays]
    both = jnp.concatenate(columns, axis=along)
    whole, at, outs = (
        lax.all_to_all(both, axis, split_axis=split_dim, concat_axis=concat_dim, tiled=True),
        0,
        [],
    )
    for a, column in zip(arrays, columns):
        slab = whole[..., at : at + column.shape[along]]
        outs.append(slab.reshape(*slab.shape[:along], *a.shape[along:]))
        at += column.shape[along]
    return tuple(outs)


def shortened(value):

    def short(part):
        return part.astype(jnp.bfloat16) if part.dtype == jnp.float32 else part

    return jax.tree.map(short, value)


def from_behind(block, axis, distance):
    devices = range(lax.axis_size(axis))
    route = [(i - distance, i) for i in devices if i - distance in devices]
    return lax.ppermute(block, axis, route)


def joined_along(tiles, dim):
    shape = list(tiles.shape[1:])
    shape[dim] *= tiles.shape[0]
    return jnp.moveaxis(tiles, 0, dim).reshape(shape)


def copy_for_each(value, axis):
    length = lax.axis_size(axis)
    return lax.all_to_all(
        jnp.broadcast_to(value[None], (length, *value.shape)), axis, 0, 0, tiled=True
    )


def gathered_copies(value, axis, dim):
    return joined_along(copy_for_each(value, axis), dim)


def in_blocks(value, dim, length):
    before, after = (value.shape[:dim], value.shape[dim + 1 :])
    return jnp.moveaxis(value.reshape(*before, length, -1, *after), dim, 0)


def sum_at_owner(value, axis, dim):
    length = lax.axis_size(axis)
    tiles = lax.all_to_all(in_blocks(value, dim, length), axis, 0, 0, tiled=True)
    return jnp.sum(tiles.astype(jnp.float32), axis=0)


def route_rows(expert_ids, home_share, experts, cap_own, cap_rep):
    half_axis = experts // 2
    capacity = cap_own + cap_rep
    flat_ids = expert_ids.reshape(-1)
    columns = jnp.arange(experts, dtype=jnp.int32)
    onehot = (flat_ids[:, None] == columns[None, :]).astype(jnp.int32)
    before = jnp.cumsum(onehot, axis=0) - onehot
    row_rank = jnp.sum(before * onehot, axis=1)
    limits = jnp.concatenate([home_share, jnp.full((experts - half_axis,), cap_own, jnp.int32)])
    home_limit = jnp.sum(onehot * limits[None, :], axis=1)
    at_home = row_rank < home_limit
    overflow = row_rank - home_limit
    to_copy = (flat_ids < half_axis) & (overflow >= 0) & (overflow < cap_rep)
    target = jnp.where(to_copy, flat_ids + half_axis, flat_ids)
    slot_index = jnp.where(to_copy, cap_own + overflow, row_rank)
    position = jnp.where(at_home | to_copy, target * capacity + slot_index, experts * capacity)
    return position.reshape(expert_ids.shape)


def expert_side(inputs, grads_out, weights_row, gate_weight, up_weight, down_weight):
    hidden_units = gate_weight.shape[1]
    gate_act = jnp.dot(inputs, gate_weight, preferred_element_type=jnp.float32)
    up_act = jnp.dot(inputs, up_weight, preferred_element_type=jnp.float32)
    sigmoid_gate = jax.nn.sigmoid(gate_act)
    silu_gate = gate_act * sigmoid_gate
    hidden = (silu_gate * up_act).astype(jnp.bfloat16)
    output = jnp.dot(hidden, down_weight, preferred_element_type=jnp.float32)
    upstream = grads_out.astype(jnp.float32)
    gate_cot = jnp.sum(upstream * output, axis=1)
    scaled = (weights_row.astype(jnp.float32)[:, None] * upstream).astype(jnp.bfloat16)
    hidden_cot = lax.dot_general(
        scaled, down_weight, (((1,), (1,)), ((), ())), preferred_element_type=jnp.float32
    )
    gate_pre = (
        hidden_cot * up_act * sigmoid_gate * (1.0 + gate_act * (1.0 - sigmoid_gate))
    ).astype(jnp.bfloat16)
    up_pre = (hidden_cot * silu_gate).astype(jnp.bfloat16)
    both_pre = jnp.concatenate([gate_pre, up_pre], axis=1)
    both_grad = lax.dot_general(
        inputs, both_pre, (((0,), (0,)), ((), ())), preferred_element_type=jnp.float32
    ).astype(jnp.bfloat16)
    grad_down = lax.dot_general(
        hidden, scaled, (((0,), (0,)), ((), ())), preferred_element_type=jnp.float32
    ).astype(jnp.bfloat16)
    return (gate_cot, both_grad[:, :hidden_units], both_grad[:, hidden_units:], grad_down)


def per_device(
    tokens, cotangent, expert_ids, gate_probs, home_share, gate_weight, up_weight, down_weight
):
    experts = lax.axis_size("expert")
    groups = lax.axis_size("dp")
    tok_rows, model_width = tokens.shape
    top_count = expert_ids.shape[1]
    cap_own = tok_rows * top_count // experts
    cap_rep = cap_own // 4
    capacity = cap_own + cap_rep
    half_axis = experts // 2
    slots_total = experts * capacity
    position = route_rows(expert_ids, home_share, experts, cap_own, cap_rep)
    spread = position.shape + (model_width,)
    row_buffer = jnp.zeros((slots_total + 1, model_width), jnp.bfloat16)
    row_buffer = row_buffer.at[position].set(jnp.broadcast_to(tokens[:, None, :], spread))
    cot_buffer = jnp.zeros((slots_total + 1, model_width), jnp.bfloat16)
    cot_buffer = cot_buffer.at[position].set(jnp.broadcast_to(cotangent[:, None, :], spread))
    prob_buffer = jnp.zeros((slots_total + 1,), jnp.bfloat16).at[position].set(gate_probs)
    send_rows = row_buffer[:-1].reshape(experts, capacity, model_width)
    send_cots = cot_buffer[:-1].reshape(experts, capacity, model_width)
    send_probs = prob_buffer[:-1].reshape(experts, capacity)
    recv_rows, recv_probs = in_one_piece((send_rows, send_probs), "expert", 0, 0, 2)
    recv_cots = lax.all_to_all(send_cots, "expert", split_axis=0, concat_axis=0, tiled=True)
    home_weights = (gate_weight[0], up_weight[0], down_weight[0])
    group_index = lax.axis_index("dp")
    pieces = tuple(
        (
            lax.dynamic_slice_in_dim(
                matrix, group_index * (matrix.shape[0] // groups), matrix.shape[0] // groups, 0
            )
            for matrix in home_weights
        )
    )
    moved_pieces = jax.tree.map(
        lambda part, own: part.astype(own.dtype),
        from_behind(shortened(pieces), "expert", half_axis),
        pieces,
    )
    copies = jax.tree.map(
        lambda part, own: part.astype(own.dtype),
        jax.tree.map(lambda part: gathered_copies(part, "dp", 0), shortened(moved_pieces)),
        moved_pieces,
    )
    own_out = expert_side(
        recv_rows[:, :cap_own].reshape(-1, model_width),
        recv_cots[:, :cap_own].reshape(-1, model_width),
        recv_probs[:, :cap_own].reshape(-1),
        home_weights[0],
        home_weights[1],
        home_weights[2],
    )
    rep_out = expert_side(
        recv_rows[:, cap_own:].reshape(-1, model_width),
        recv_cots[:, cap_own:].reshape(-1, model_width),
        recv_probs[:, cap_own:].reshape(-1),
        copies[0],
        copies[1],
        copies[2],
    )
    gate_cot = jnp.concatenate(
        [own_out[0].reshape(experts, cap_own), rep_out[0].reshape(experts, cap_rep)], axis=1
    )
    returned = lax.all_to_all(gate_cot, "expert", split_axis=0, concat_axis=0, tiled=True)
    gate_grads = jnp.concatenate([returned.reshape(-1), jnp.zeros((1,), jnp.float32)])[position]
    own_bf = own_out[1:]
    copy_bf = rep_out[1:]
    sent_home = jax.tree.map(
        lambda part, own: part.astype(own.dtype),
        from_behind(shortened(copy_bf), "expert", -half_axis),
        copy_bf,
    )
    device_terms = tuple(
        (
            local_part.astype(jnp.float32) + remote_part.astype(jnp.float32)
            for local_part, remote_part in zip(own_bf, sent_home)
        )
    )
    summed = jax.tree.map(lambda part: sum_at_owner(part, "dp", 0), shortened(device_terms))
    return (gate_grads, summed[0][None], summed[1][None], summed[2][None])


def solution(mesh):
    return jax.shard_map(
        per_device,
        mesh=mesh,
        in_specs=(
            P(("dp", "expert"), None),
            P(("dp", "expert"), None),
            P(("dp", "expert"), None),
            P(("dp", "expert"), None),
            P(),
            P("expert", None, None),
            P("expert", None, None),
            P("expert", None, None),
        ),
        out_specs=(
            P(("dp", "expert"), None),
            P("expert", "dp", None),
            P("expert", "dp", None),
            P("expert", "dp", None),
        ),
        check_vma=False,
    )
```

profile of v0, /device:TPU:65, one launch (start us, length us, event | category | flops | bytes accessed | tf_op | source)
XLA Modules:
  0.0 637.7 jit_solution(5765846346829331890)
XLA Ops:
  1.5 18.2 %collective-permute-start.2 = (bf16[24,1024]{1,0:T(8,128)(2,1)S(1)}, bf16[24,1024]{1,0:T(8,128)(2,1)S(1)}, u32[]{:S(2)}, u32[]{:S(2)}) collective-permute-start(bf16[24,1024]{1,0:T(8,128)(2,1)S(1)} %dynamic-slice_bitcast_fusion), channel_id=1, source_target_pairs={{0,32},{1,33},{2,34},{3,35},{4,36},{5,37},{6,38},{7,39},{8,40},{9,... | collective-permute-start | bytes 147464 | tf_op jit(solution)/shard_map/ppermute | solution.py:33
  21.8 8.6 %all-to-all-start.4 = ((bf16[16,24,1024]{2,1,0:T(8,128)(2,1)}), bf16[16,24,1024]{2,1,0:T(8,128)(2,1)S(1)}, u32[]{:S(2)}, u32[]{:S(2)}) async-start(bf16[16,24,1024]{2,1,0:T(8,128)(2,1)} %broadcast_in_dim.31), calls=%async_computation.4 | async-start | bytes 1572864 | tf_op jit(solution)/shard_map/all_to_all | solution.py:44
  31.3 12.8 %collective-permute-start.1 = (bf16[64,384]{1,0:T(8,128)(2,1)S(1)}, bf16[64,384]{1,0:T(8,128)(2,1)S(1)}, u32[]{:S(2)}, u32[]{:S(2)}) collective-permute-start(bf16[64,384]{1,0:T(8,128)(2,1)S(1)} %dynamic-slice_bitcast_fusion.1), channel_id=1, source_target_pairs={{0,32},{1,33},{2,34},{3,35},{4,36},{5,37},{6,38},{7,39},{8,40},{9,... | collective-permute-start | bytes 147464 | tf_op jit(solution)/shard_map/ppermute | solution.py:33
  44.1 1.2 collective-permute-done.1
  45.3 7.9 %all-to-all-done.4 = bf16[16,24,1024]{2,1,0:T(8,128)(2,1)S(1)} async-done(((bf16[16,24,1024]{2,1,0:T(8,128)(2,1)}), bf16[16,24,1024]{2,1,0:T(8,128)(2,1)S(1)}, u32[]{:S(2)}, u32[]{:S(2)}) %all-to-all-start.4) | async-done | bytes 786464 | tf_op jit(solution)/shard_map/all_to_all | solution.py:44
  54.3 4.3 all-to-all-start.3
  59.0 1.2 reduce-window.6
  61.9 2.9 scatter_custom_fusion
  64.9 1.6 reshape.118
  66.5 13.8 %all-to-all-done.3 = bf16[16,64,384]{2,1,0:T(8,128)(2,1)} async-done(((bf16[16,64,384]{2,1,0:T(8,128)(2,1)}), bf16[16,64,384]{2,1,0:T(8,128)(2,1)}, u32[]{:S(2)}, u32[]{:S(2)}) %all-to-all-start.3) | async-done | bytes 786464 | tf_op jit(solution)/shard_map/all_to_all | solution.py:44
  80.3 17.0 %all-to-all-start = ((bf16[64,10,1024]{2,1,0:T(8,128)(2,1)}), bf16[64,10,1024]{2,1,0:T(8,128)(2,1)}, u32[]{:S(2)}, u32[]{:S(2)}) async-start(bf16[64,10,1024]{2,1,0:T(8,128)(2,1)} %reshape.118), calls=%async_computation | async-start | bytes 4194304 | tf_op jit(solution)/shard_map/all_to_all | solution.py:134
  97.6 3.9 scatter_custom_fusion.2
  103.2 3.6 scatter_custom_fusion.1
  106.8 1.2 slice.72
  108.0 2.4 reshape.119
  110.3 1.8 pad_maximum_fusion
  112.1 83.1 %all-to-all-done = bf16[64,10,1024]{2,1,0:T(8,128)(2,1)} async-done(((bf16[64,10,1024]{2,1,0:T(8,128)(2,1)}), bf16[64,10,1024]{2,1,0:T(8,128)(2,1)}, u32[]{:S(2)}, u32[]{:S(2)}) %all-to-all-start) | async-done | bytes 1310752 | tf_op jit(solution)/shard_map/all_to_all | solution.py:134
  195.2 6.9 %all-to-all-start.1 = ((bf16[64,10,1025]{2,1,0:T(8,128)(2,1)}), bf16[64,10,1025]{2,1,0:T(8,128)(2,1)S(1)}, u32[]{:S(2)}, u32[]{:S(2)}) async-start(bf16[64,10,1025]{2,1,0:T(8,128)(2,1)} %pad_maximum_fusion), calls=%async_computation.1 | async-start | bytes 4718592 | tf_op jit(solution)/shard_map/all_to_all | solution.py:11
  202.2 11.0 %collective-permute-start = (bf16[64,384]{1,0:T(8,128)(2,1)S(1)}, bf16[64,384]{1,0:T(8,128)(2,1)S(1)}, u32[]{:S(2)}, u32[]{:S(2)}) collective-permute-start(bf16[64,384]{1,0:T(8,128)(2,1)S(1)} %dynamic-slice_bitcast_fusion.2), channel_id=1, source_target_pairs={{0,32},{1,33},{2,34},{3,35},{4,36},{5,37},{6,38},{7,39},{8,40},{9,... | collective-permute-start | bytes 147464 | tf_op jit(solution)/shard_map/ppermute | solution.py:33
  213.2 89.0 %collective-permute-done = bf16[64,384]{1,0:T(8,128)(2,1)S(1)} collective-permute-done((bf16[64,384]{1,0:T(8,128)(2,1)S(1)}, bf16[64,384]{1,0:T(8,128)(2,1)S(1)}, u32[]{:S(2)}, u32[]{:S(2)}) %collective-permute-start) | collective-permute-done | bytes 49184 | tf_op jit(solution)/shard_map/ppermute | solution.py:33
  302.2 10.0 %all-to-all-done.1 = bf16[64,10,1025]{2,1,0:T(8,128)(2,1)S(1)} async-done(((bf16[64,10,1025]{2,1,0:T(8,128)(2,1)}), bf16[64,10,1025]{2,1,0:T(8,128)(2,1)S(1)}, u32[]{:S(2)}, u32[]{:S(2)}) %all-to-all-start.1) | async-done | bytes 1312032 | tf_op jit(solution)/shard_map/all_to_all | solution.py:11
  313.4 5.0 all-to-all-start.2
  318.4 2.2 slice_convert_fusion
  320.6 1.4 reshape.133
  322.6 1.5 slice.75
  324.2 1.5 multiply_convert_fusion.4
  325.8 1.4 fusion.45
  327.7 13.5 %all-to-all-done.2 = bf16[16,64,384]{2,1,0:T(8,128)(2,1)} async-done(((bf16[16,64,384]{2,1,0:T(8,128)(2,1)}), bf16[16,64,384]{2,1,0:T(8,128)(2,1)}, u32[]{:S(2)}, u32[]{:S(2)}) %all-to-all-start.2) | async-done | bytes 786464 | tf_op jit(solution)/shard_map/all_to_all | solution.py:44
  341.2 2.3 multiply_convert_fusion.7
  343.9 1.4 collective-permute-start.5
  345.4 1.5 fusion.12
  346.9 2.8 fusion.7
  350.3 3.6 multiply_convert_fusion.1
  354.0 2.0 fusion.2
  356.8 16.0 %all-to-all-start.5 = ((f32[64,1,10]{2,1,0:T(1,128)}), f32[64,1,10]{2,1,0:T(1,128)S(1)}, u32[]{:S(2)}, u32[]{:S(2)}) async-start(f32[64,1,10]{2,1,0:T(1,128)} %bitcast.13), calls=%async_computation.5 | async-start | bytes 65536 | tf_op jit(solution)/shard_map/all_to_all | solution.py:174
  372.8 51.7 %collective-permute-done.5 = bf16[384,1024]{1,0:T(8,128)(2,1)} collective-permute-done((bf16[384,1024]{1,0:T(8,128)(2,1)S(1)}, bf16[384,1024]{1,0:T(8,128)(2,1)}, u32[]{:S(2)}, u32[]{:S(2)}) %collective-permute-start.5) | collective-permute-done | bytes 786464 | tf_op jit(solution)/shard_map/ppermute | solution.py:33
  424.4 3.0 add_convert_fusion
  427.5 4.9 all-to-all-start.8
  433.2 1.4 collective-permute-start.4
  434.6 1.3 collective-permute-start.3
  437.0 126.3 %collective-permute-done.4 = bf16[1024,384]{1,0:T(8,128)(2,1)S(1)} collective-permute-done((bf16[1024,384]{1,0:T(8,128)(2,1)S(1)}, bf16[1024,384]{1,0:T(8,128)(2,1)S(1)}, u32[]{:S(2)}, u32[]{:S(2)}) %collective-permute-start.4) | collective-permute-done | bytes 786464 | tf_op jit(solution)/shard_map/ppermute | solution.py:33
  563.3 16.9 %collective-permute-done.3 = bf16[1024,384]{1,0:T(8,128)(2,1)S(1)} collective-permute-done((bf16[1024,384]{1,0:T(8,128)(2,1)S(1)}, bf16[1024,384]{1,0:T(8,128)(2,1)S(1)}, u32[]{:S(2)}, u32[]{:S(2)}) %collective-permute-start.3) | collective-permute-done | bytes 786464 | tf_op jit(solution)/shard_map/ppermute | solution.py:33
  580.1 1.3 add_convert_fusion.1
  581.4 30.0 %all_to_all.49 = bf16[16,64,384]{2,1,0:T(8,128)(2,1)} all-to-all(bf16[16,64,384]{2,1,0:T(8,128)(2,1)S(1)} %bitcast.90), channel_id=1, replica_groups=mesh['dp'=16,'expert'=64] {'dp'}, dimensions={0} | all-to-all | bytes 1572864 | tf_op jit(solution)/shard_map/all_to_all | solution.py:60
  611.4 3.5 all-to-all-start.7
  616.4 2.3 gather_fusion
  620.2 1.9 convert_reduce_fusion.2
  622.1 14.9 %all-to-all-done.7 = bf16[16,64,384]{2,1,0:T(8,128)(2,1)S(1)} async-done(((bf16[16,64,384]{2,1,0:T(8,128)(2,1)}), bf16[16,64,384]{2,1,0:T(8,128)(2,1)S(1)}, u32[]{:S(2)}, u32[]{:S(2)}) %all-to-all-start.7) | async-done | bytes 786464 | tf_op jit(solution)/shard_map/all_to_all | solution.py:60
  (96 shorter events, 18.5 us)
Async XLA Ops:
  0.6 201.5 %copy-start = (bf16[1,1024,384]{2,1,0:T(8,128)(2,1)S(1)}, bf16[1,1024,384]{2,1,0:T(8,128)(2,1)}, u32[]{:S(2)}) copy-start(bf16[1,1024,384]{2,1,0:T(8,128)(2,1)} %param.13) | copy-start | bytes 2359300
  1.5 19.3 %collective-permute-start.2 = (bf16[24,1024]{1,0:T(8,128)(2,1)S(1)}, bf16[24,1024]{1,0:T(8,128)(2,1)S(1)}, u32[]{:S(2)}, u32[]{:S(2)}) collective-permute-start(bf16[24,1024]{1,0:T(8,128)(2,1)S(1)} %dynamic-slice_bitcast_fusion), channel_id=1, source_target_pairs={{0,32},{1,33},{2,34},{3,35},{4,36},{5,37},{6,38},{7,39},{8,40},{9,... | collective-permute-start | bytes 147464 | tf_op jit(solution)/shard_map/ppermute | solution.py:33
  21.8 31.4 %all-to-all-start.4 = ((bf16[16,24,1024]{2,1,0:T(8,128)(2,1)}), bf16[16,24,1024]{2,1,0:T(8,128)(2,1)S(1)}, u32[]{:S(2)}, u32[]{:S(2)}) async-start(bf16[16,24,1024]{2,1,0:T(8,128)(2,1)} %broadcast_in_dim.31), calls=%async_computation.4 | async-start | bytes 1572864 | tf_op jit(solution)/shard_map/all_to_all | solution.py:44
  30.5 28.2 %copy-start.9 = (s32[128,4]{0,1:T(4,128)S(1)}, s32[128,4]{0,1:T(4,128)}, u32[]{:S(2)}) copy-start(s32[128,4]{0,1:T(4,128)} %param.10) | copy-start | bytes 6148
  31.3 29.2 %copy-start.14 = (s32[32]{0:T(128)S(1)}, s32[32]{0:T(128)}, u32[]{:S(2)}) copy-start(s32[32]{0:T(128)} %param.12) | copy-start | bytes 388
  31.3 14.0 %collective-permute-start.1 = (bf16[64,384]{1,0:T(8,128)(2,1)S(1)}, bf16[64,384]{1,0:T(8,128)(2,1)S(1)}, u32[]{:S(2)}, u32[]{:S(2)}) collective-permute-start(bf16[64,384]{1,0:T(8,128)(2,1)S(1)} %dynamic-slice_bitcast_fusion.1), channel_id=1, source_target_pairs={{0,32},{1,33},{2,34},{3,35},{4,36},{5,37},{6,38},{7,39},{8,40},{9,... | collective-permute-start | bytes 147464 | tf_op jit(solution)/shard_map/ppermute | solution.py:33
  53.2 7.3 %copy-start.1 = (bf16[16,24,1024]{2,1,0:T(8,128)(2,1)}, bf16[16,24,1024]{2,1,0:T(8,128)(2,1)S(1)}, u32[]{:S(2)}) copy-start(bf16[16,24,1024]{2,1,0:T(8,128)(2,1)S(1)} %all-to-all-done.4) | copy-start | bytes 2359300
  54.3 6.9 %copy-start.6 = (bf16[128,1024]{1,0:T(8,128)(2,1)S(1)}, bf16[128,1024]{1,0:T(8,128)(2,1)}, u32[]{:S(2)}) copy-start(bf16[128,1024]{1,0:T(8,128)(2,1)} %param.9) | copy-start | bytes 786436
  54.3 26.0 %all-to-all-start.3 = ((bf16[16,64,384]{2,1,0:T(8,128)(2,1)}), bf16[16,64,384]{2,1,0:T(8,128)(2,1)}, u32[]{:S(2)}, u32[]{:S(2)}) async-start(bf16[16,64,384]{2,1,0:T(8,128)(2,1)} %broadcast_in_dim.30), calls=%async_computation.3 | async-start | bytes 1572864 | tf_op jit(solution)/shard_map/all_to_all | solution.py:44
  66.5 30.8 %copy-start.13 = (bf16[128,4]{0,1:T(4,128)(2,1)S(1)}, bf16[128,4]{0,1:T(4,128)(2,1)}, u32[]{:S(2)}) copy-start(bf16[128,4]{0,1:T(4,128)(2,1)} %param.11) | copy-start | bytes 3076
  66.5 35.3 %copy-start.7 = (bf16[128,1024]{1,0:T(8,128)(2,1)S(1)}, bf16[128,1024]{1,0:T(8,128)(2,1)}, u32[]{:S(2)}) copy-start(bf16[128,1024]{1,0:T(8,128)(2,1)} %param.8) | copy-start | bytes 786436
  80.3 114.9 %all-to-all-start = ((bf16[64,10,1024]{2,1,0:T(8,128)(2,1)}), bf16[64,10,1024]{2,1,0:T(8,128)(2,1)}, u32[]{:S(2)}, u32[]{:S(2)}) async-start(bf16[64,10,1024]{2,1,0:T(8,128)(2,1)} %reshape.118), calls=%async_computation | async-start | bytes 4194304 | tf_op jit(solution)/shard_map/all_to_all | solution.py:134
  195.2 117.0 %all-to-all-start.1 = ((bf16[64,10,1025]{2,1,0:T(8,128)(2,1)}), bf16[64,10,1025]{2,1,0:T(8,128)(2,1)S(1)}, u32[]{:S(2)}, u32[]{:S(2)}) async-start(bf16[64,10,1025]{2,1,0:T(8,128)(2,1)} %pad_maximum_fusion), calls=%async_computation.1 | async-start | bytes 4718592 | tf_op jit(solution)/shard_map/all_to_all | solution.py:11
  202.2 100.0 %collective-permute-start = (bf16[64,384]{1,0:T(8,128)(2,1)S(1)}, bf16[64,384]{1,0:T(8,128)(2,1)S(1)}, u32[]{:S(2)}, u32[]{:S(2)}) collective-permute-start(bf16[64,384]{1,0:T(8,128)(2,1)S(1)} %dynamic-slice_bitcast_fusion.2), channel_id=1, source_target_pairs={{0,32},{1,33},{2,34},{3,35},{4,36},{5,37},{6,38},{7,39},{8,40},{9,... | collective-permute-start | bytes 147464 | tf_op jit(solution)/shard_map/ppermute | solution.py:33
  312.3 6.1 copy-start.3
  313.4 27.8 %all-to-all-start.2 = ((bf16[16,64,384]{2,1,0:T(8,128)(2,1)}), bf16[16,64,384]{2,1,0:T(8,128)(2,1)}, u32[]{:S(2)}, u32[]{:S(2)}) async-start(bf16[16,64,384]{2,1,0:T(8,128)(2,1)} %broadcast_in_dim.29), calls=%async_computation.2 | async-start | bytes 1572864 | tf_op jit(solution)/shard_map/all_to_all | solution.py:44
  320.6 1.5 slice-start
  322.6 4.6 copy-start.2
  341.2 4.2 copy-start.4
  341.2 4.2 copy-start.10
  343.9 3.0 copy-start.11
  343.9 80.5 %collective-permute-start.5 = (bf16[384,1024]{1,0:T(8,128)(2,1)S(1)}, bf16[384,1024]{1,0:T(8,128)(2,1)}, u32[]{:S(2)}, u32[]{:S(2)}) collective-permute-start(bf16[384,1024]{1,0:T(8,128)(2,1)S(1)} %convolution_convert_fusion.2), channel_id=1, source_target_pairs={{32,0},{33,1},{34,2},{35,3},{36,4},{37,5},{38,6},{39,7},{40,8},{41... | collective-permute-start | bytes 2359304 | tf_op jit(solution)/shard_map/ppermute | solution.py:33
  350.3 3.6 copy-start.12
  356.8 70.7 %all-to-all-start.5 = ((f32[64,1,10]{2,1,0:T(1,128)}), f32[64,1,10]{2,1,0:T(1,128)S(1)}, u32[]{:S(2)}, u32[]{:S(2)}) async-start(f32[64,1,10]{2,1,0:T(1,128)} %bitcast.13), calls=%async_computation.5 | async-start | bytes 65536 | tf_op jit(solution)/shard_map/all_to_all | solution.py:174
  427.5 4.9 copy-start.8
  427.5 153.9 %all-to-all-start.8 = ((bf16[16,24,1024]{2,1,0:T(8,128)(2,1)}), bf16[16,24,1024]{2,1,0:T(8,128)(2,1)S(1)}, u32[]{:S(2)}, u32[]{:S(2)}) async-start(bf16[16,24,1024]{2,1,0:T(8,128)(2,1)} %bitcast.20), calls=%async_computation.8 | async-start | bytes 1572864 | tf_op jit(solution)/shard_map/all_to_all | solution.py:60
  433.0 2.9 copy-start.5
  433.0 2.9 copy-start.15
  433.0 2.9 copy-start.16
  433.2 130.1 %collective-permute-start.4 = (bf16[1024,384]{1,0:T(8,128)(2,1)S(1)}, bf16[1024,384]{1,0:T(8,128)(2,1)S(1)}, u32[]{:S(2)}, u32[]{:S(2)}) collective-permute-start(bf16[1024,384]{1,0:T(8,128)(2,1)S(1)} %get-tuple-element.28), channel_id=1, source_target_pairs={{32,0},{33,1},{34,2},{35,3},{36,4},{37,5},{38,6},{39,7},{40,8},{41... | collective-permute-start | bytes 2359304 | tf_op jit(solution)/shard_map/ppermute | solution.py:33
  434.6 145.5 %collective-permute-start.3 = (bf16[1024,384]{1,0:T(8,128)(2,1)S(1)}, bf16[1024,384]{1,0:T(8,128)(2,1)S(1)}, u32[]{:S(2)}, u32[]{:S(2)}) collective-permute-start(bf16[1024,384]{1,0:T(8,128)(2,1)S(1)} %get-tuple-element.29), channel_id=1, source_target_pairs={{32,0},{33,1},{34,2},{35,3},{36,4},{37,5},{38,6},{39,7},{40,8},{41... | collective-permute-start | bytes 2359304 | tf_op jit(solution)/shard_map/ppermute | solution.py:33
  611.4 25.5 %all-to-all-start.7 = ((bf16[16,64,384]{2,1,0:T(8,128)(2,1)}), bf16[16,64,384]{2,1,0:T(8,128)(2,1)S(1)}, u32[]{:S(2)}, u32[]{:S(2)}) async-start(bf16[16,64,384]{2,1,0:T(8,128)(2,1)} %bitcast.18), calls=%async_computation.7 | async-start | bytes 1572864 | tf_op jit(solution)/shard_map/all_to_all | solution.py:60
where the time goes:
time: 639 us; the launch traced here: 638 us
  waiting for transfers between devices  429 us (67%)
  starting transfers between devices  112 us (18%)
  local copies, waits for them, and re-layouts  32.1 us (5%)
  blocking collectives  30 us (5%)
  matrix products  19.5 us (3%)
  other arithmetic  13 us (2%)
    ppermute x6, waiting for transfers between devices, from_behind(): return lax.ppermute(block, axis, route)  286 us
    all_to_all x1, waiting for transfers between devices, per_device(): lax.all_to_all(send_cots, 'expert', split_axis=0, concat_axis=0, tiled=True)  83.1 us
    ppermute x6, starting transfers between devices, from_behind(): return lax.ppermute(block, axis, route)  46.1 us
    all_to_all x3, waiting for transfers between devices, copy_for_each(): lax.all_to_all(jnp.broadcast_to(value[None], (length, *value.shape)), axi...  35.3 us
    all_to_all x1, blocking collectives, sum_at_owner(): lax.all_to_all(in_blocks(value, dim, length), axis, 0, 0, tiled=True)  30 us
    all_to_all x3, starting transfers between devices, copy_for_each(): lax.all_to_all(jnp.broadcast_to(value[None], (length, *value.shape)), axi...  17.9 us
    all_to_all x1, starting transfers between devices, per_device(): lax.all_to_all(send_cots, 'expert', split_axis=0, concat_axis=0, tiled=True)  17 us
    all_to_all x1, starting transfers between devices, per_device(): lax.all_to_all(gate_cot, 'expert', split_axis=0, concat_axis=0, tiled=True)  16 us
  transfers between devices with their start and end apart: 14, of which 12 were waited for; matrix products, arithmetic and copies ran while one was open for 9% of the time, Pallas kernels for 0%

commit v1 on v0

v1 whole, which is shorter than its diff:
```python
import functools

import jax
import jax.numpy as jnp
from jax import lax
from jax.experimental import pallas as pl
from jax.experimental.pallas import tpu as pltpu
from jax.sharding import PartitionSpec as P

MESH = pl.DeviceIdType.MESH
CAP_OWN = 8
CAP_REP = 2
NX = 4
DROPPED = 99.0
F32 = jnp.float32
BF16 = jnp.bfloat16
VMEM = pl.BlockSpec(memory_space=pltpu.VMEM)
ANY = pl.BlockSpec(memory_space=pl.ANY)


def dot(a, b, dims=((1,), (0,))):
    return lax.dot_general(a, b, (dims, ((), ())), preferred_element_type=F32)


def pack_kernel(ids_ref, prob_ref, cap_ref, tok_ref, cot_ref, base_ref, ext_ref, rank_ref, pw_ref):
    experts, toks = rank_ref.shape
    half, _, wide = ext_ref.shape
    row = lax.broadcasted_iota(jnp.int32, (experts, toks), 0)
    named = jnp.zeros((experts, toks), F32)
    weight = jnp.zeros((experts, toks), F32)
    for k in range(ids_ref.shape[0]):
        hit = ids_ref[k : k + 1, :] == row
        named += jnp.where(hit, 1.0, 0.0)
        weight += jnp.where(hit, prob_ref[k : k + 1, :], 0.0)
    earlier = lax.broadcasted_iota(jnp.int32, (toks, toks), 0) < lax.broadcasted_iota(jnp.int32, (toks, toks), 1)
    before = dot(named.astype(BF16), jnp.where(earlier, 1.0, 0.0).astype(BF16))
    kept = (named > 0.5) & (before < cap_ref[...])
    rank_ref[...] = jnp.where(kept, before, DROPPED)
    pw_ref[...] = weight

    group = 8

    @pl.loop(0, experts // group)
    def _(b):
        at = pl.ds(pl.multiple_of(b * group, group), group)
        shape = (group, 16, toks)
        slot = lax.broadcasted_iota(jnp.int32, shape, 1).astype(F32)
        ranks = jnp.broadcast_to(rank_ref[at, :].reshape(group, 1, toks), shape)
        weights = jnp.broadcast_to(pw_ref[at, :].reshape(group, 1, toks), shape)
        pick = jnp.where((ranks == slot) & (slot < 7.5), 1.0, 0.0).reshape(group * 16, toks).astype(BF16)
        scale = jnp.where(ranks == slot - 8.0, weights, 0.0).reshape(group * 16, toks).astype(BF16)
        rows = dot(pick, tok_ref[...]) + dot(scale, cot_ref[...])
        base_ref[at] = rows.reshape(group, 16, rows.shape[1]).astype(BF16)

    big = 16 if half % 16 == 0 else half

    @pl.loop(0, half // big)
    def _(b):
        at = pl.ds(pl.multiple_of(b * big, big), big)
        shape = (big, 8, toks)
        place = lax.broadcasted_iota(jnp.int32, shape, 1)
        ranks = jnp.broadcast_to(rank_ref[at, :].reshape(big, 1, toks), shape)
        weights = jnp.broadcast_to(pw_ref[at, :].reshape(big, 1, toks), shape)
        here = ranks == (8 + place % 2).astype(F32)
        total = jnp.zeros((big * 8, wide), F32)
        for q in range(2):
            pick = jnp.where(here & (place // 2 == 2 * q), 1.0, 0.0).reshape(big * 8, toks).astype(BF16)
            scale = jnp.where(here & (place // 2 == 2 * q + 1), weights, 0.0).reshape(big * 8, toks).astype(BF16)
            cols = slice(q * wide, (q + 1) * wide)
            total += dot(pick, tok_ref[:, cols]) + dot(scale, cot_ref[:, cols])
        ext_ref[at] = total.reshape(big, 8, wide).astype(BF16)


def partner(k, nz, zx):
    z, x = zx
    j = k // NX
    odd = j % 2
    dz = nz // 2 + (1 - odd) * (j // 2) - odd * ((j + 1) // 2)
    pz = lax.rem(z + dz + nz, nz)
    px = lax.rem(x + lax.rem(k, NX) + 1, NX)
    return pz, px


def send_kernel(nz, base_ref, ext_ref, rb_ref, re_ref, bsend, brecv, esend, erecv, lsem):
    me = lax.axis_index("expert")
    zx = (me // NX, lax.rem(me, NX))
    experts = nz * NX
    half = experts // 2
    low = me < half
    barrier = pltpu.get_barrier_semaphore()

    def greet(k, c):
        pz, px = partner(k, nz, zx)
        pl.semaphore_signal(barrier, inc=1, device_id={"expert": pz * NX + px}, device_id_type=MESH)
        return c

    lax.fori_loop(0, experts - 1, greet, 0)
    own = pltpu.make_async_copy(base_ref.at[me], rb_ref.at[me], lsem.at[0])
    own.start()
    pl.semaphore_wait(barrier, experts - 1)

    def base_copy(k, peer):
        return pltpu.make_async_remote_copy(
            src_ref=base_ref.at[peer],
            dst_ref=rb_ref.at[me],
            send_sem=bsend.at[k],
            recv_sem=brecv.at[k],
            device_id={"expert": peer},
            device_id_type=MESH,
        )

    def ext_copy(k, peer):
        return pltpu.make_async_remote_copy(
            src_ref=ext_ref.at[peer],
            dst_ref=re_ref.at[me],
            send_sem=esend.at[k],
            recv_sem=erecv.at[k],
            device_id={"expert": peer},
            device_id_type=MESH,
        )

    def issue(k, c):
        pz, px = partner(k, nz, zx)
        peer = pz * NX + px
        base_copy(k, peer).start()

        @pl.when(peer < half)
        def _():
            ext_copy(k, peer).start()

        return c

    lax.fori_loop(0, experts - 1, issue, 0)

    @pl.when(low)
    def _():
        mine = pltpu.make_async_copy(ext_ref.at[me], re_ref.at[me], lsem.at[1])
        mine.start()
        mine.wait()

    def finish(k, c):
        pz, px = partner(k, nz, zx)
        peer = pz * NX + px
        base_copy(k, peer).wait()

        @pl.when(peer < half)
        def _():
            ext_copy(k, peer).wait_send()

        @pl.when(low)
        def _():
            ext_copy(k, 0).wait_recv()

        return c

    lax.fori_loop(0, experts - 1, finish, 0)
    own.wait()


def expert_kernel(
    flag_ref, rb_ref, re_ref, wg_ref, wu_ref, wd_ref,
    gate_ref, up_ref, dl_ref, dr_ref, v_ref,
    x_ref, s_ref, h_ref, pg_ref, pu_ref, ve_ref,
):
    sources, _, d = rb_ref.shape
    wide = d // 2
    ff = wg_ref.shape[1]
    base = sources * 8
    block = 128
    low = flag_ref[0] > 0

    @pl.loop(0, base // block)
    def _(b):
        part = rb_ref[pl.ds(b * (block // 8), block // 8)].astype(F32)
        at = pl.ds(pl.multiple_of(b * block, block), block)
        x_ref[at, :] = part[:, :8, :].reshape(block, d).astype(BF16)
        s_ref[at, :] = part[:, 8:, :].reshape(block, d).astype(BF16)

    extra = re_ref[...].astype(F32).reshape(sources * 8, wide)
    extra = jnp.where(low, extra, 0.0).astype(BF16)
    out_row = lax.broadcasted_iota(jnp.int32, (4 * sources, sources * 8), 0)
    in_row = lax.broadcasted_iota(jnp.int32, (4 * sources, sources * 8), 1)
    wanted = (out_row % sources) * 8 + out_row // sources
    for q in range(2):
        pick = jnp.where(in_row == wanted + 4 * q, 1.0, 0.0).astype(BF16)
        rows = dot(pick, extra).astype(BF16)
        cols = slice(q * wide, (q + 1) * wide)
        x_ref[base : base + 2 * sources, cols] = rows[: 2 * sources]
        s_ref[base : base + 2 * sources, cols] = rows[2 * sources :]

    def side(at, rows):
        x, s = x_ref[at, :], s_ref[at, :]
        a = dot(x, wg_ref[...])
        b = dot(x, wu_ref[...])
        sig = jax.nn.sigmoid(a)
        silu = a * sig
        hidden = (silu * b).astype(BF16)
        h_ref[at, :] = hidden
        cot = dot(s, wd_ref[...], ((1,), (1,)))
        pg_ref[at, :] = (cot * b * sig * (1.0 + a * (1.0 - sig))).astype(BF16)
        pu_ref[at, :] = (cot * silu).astype(BF16)
        out = dot(hidden, wd_ref[...])
        return jnp.sum(out * s.astype(F32), axis=1, keepdims=True)

    col = side(pl.ds(base, 2 * sources), 2 * sources)
    lane = lax.broadcasted_iota(jnp.int32, (sources, 128), 1)
    ve_ref[...] = jnp.where(lane == 8, col[:sources], 0.0) + jnp.where(lane == 9, col[sources:], 0.0)

    @pl.loop(0, base // block)
    def _(b):
        at = pl.ds(pl.multiple_of(b * block, block), block)
        col = side(at, block)
        few = block // 8
        shape = (block, 128)
        lane = lax.broadcasted_iota(jnp.int32, shape, 1)
        sub = lax.broadcasted_iota(jnp.int32, shape, 0) % 8
        tile = jnp.where(lane == sub, col, 0.0).reshape(few, 8, 128)
        src = pl.ds(pl.multiple_of(b * few, few), few)
        extra = jnp.broadcast_to(ve_ref[src, :].reshape(few, 1, 128), (few, 8, 128))
        first = lax.broadcasted_iota(jnp.int32, (few, 8, 128), 1) == 0
        v_ref[src] = tile + jnp.where(first, extra, 0.0)

    ny, _, share, _ = gate_ref.shape
    turn = (((0,), (0,)))
    for y in range(ny):
        xs = x_ref[:, y * 2 * share : (y + 1) * 2 * share]
        gate_ref[y] = dot(xs, pg_ref[...], turn).reshape(2, share, ff).astype(BF16)
        up_ref[y] = dot(xs, pu_ref[...], turn).reshape(2, share, ff).astype(BF16)
    few = dl_ref.shape[2]
    pair = ny * 2 * few
    step = min(128, pair)
    for side_ref, at in ((dl_ref, 0), (dr_ref, wide)):
        down = dot(h_ref[...], s_ref[:, at : at + wide], turn)
        side_ref[...] = down.reshape(ny, 2, few, wide).astype(BF16)


def ring_kernel(
    nz, ids_ref, prob_ref, rank_ref, v_ref, gate_ref, up_ref, dl_ref, dr_ref,
    gc_out, gate_out, up_out, down_out,
    vr_ref, peer_g, peer_u, peer_l, peer_r,
    out_g, out_u, out_l, out_r, in_g, in_u, in_l, in_r,
    vsend, vrecv, dsend, drecv, rsend, rrecv,
):
    me = lax.axis_index("expert")
    zx = (me // NX, lax.rem(me, NX))
    experts = nz * NX
    dp = lax.axis_index("dp")
    y, core = dp // 2, lax.rem(dp, 2)
    ny = gate_ref.shape[0]
    barrier = pltpu.get_barrier_semaphore()
    other = 1 - core
    ahead = lax.rem(y + 1, ny) * 2 + core
    behind = lax.rem(y + ny - 1, ny) * 2 + core

    def greet(k, c):
        pz, px = partner(k, nz, zx)
        pl.semaphore_signal(barrier, inc=1, device_id={"expert": pz * NX + px}, device_id_type=MESH)
        return c

    for near in (y * 2 + other, ahead, behind):
        pl.semaphore_signal(barrier, inc=1, device_id={"dp": near}, device_id_type=MESH)
    lax.fori_loop(0, experts - 1, greet, 0)
    pl.semaphore_wait(barrier, experts - 1 + 3)

    parts = (
        (gate_ref, peer_g, out_g, in_g, 1),
        (up_ref, peer_u, out_u, in_u, -1),
        (dl_ref, peer_l, out_l, in_l, 1),
        (dr_ref, peer_r, out_r, in_r, -1),
    )

    def owner(way, s):
        return lax.rem(y - way * (1 + s) + 2 * ny, ny)

    def across(i, s):
        src, dst, _, _, way = parts[i]
        o = owner(way, s)
        return pltpu.make_async_remote_copy(
            src_ref=src.at[o, other],
            dst_ref=dst.at[o],
            send_sem=dsend.at[i, s],
            recv_sem=drecv.at[i, s],
            device_id={"dp": y * 2 + other},
            device_id_type=MESH,
        )

    for s in range(ny):
        for i in range(4):
            across(i, s).start()

    def v_copy(k):
        pz, px = partner(k, nz, zx)
        peer = pz * NX + px
        return pltpu.make_async_remote_copy(
            src_ref=v_ref.at[peer],
            dst_ref=vr_ref.at[me],
            send_sem=vsend.at[k],
            recv_sem=vrecv.at[k],
            device_id={"expert": peer},
            device_id_type=MESH,
        )

    def v_issue(k, c):
        v_copy(k).start()
        return c

    lax.fori_loop(0, experts - 1, v_issue, 0)
    vr_ref[pl.ds(me, 1)] = v_ref[pl.ds(me, 1)]

    def hop(i, s):
        _, _, out, inn, way = parts[i]
        return pltpu.make_async_remote_copy(
            src_ref=out.at[s],
            dst_ref=inn.at[s],
            send_sem=rsend.at[i, s],
            recv_sem=rrecv.at[i, s],
            device_id={"dp": ahead if way == 1 else behind},
            device_id_type=MESH,
        )

    def local(i, s):
        src, dst, _, _, way = parts[i]
        o = owner(way, s)
        across(i, s).wait()
        return src[o, core].astype(F32) + dst[o].astype(F32)

    for s in range(ny - 1):
        for i in range(4):
            _, _, out, inn, _ = parts[i]
            total = local(i, s)
            if s > 0:
                hop(i, s - 1).wait_recv()
                total = total + inn[s - 1].astype(F32)
            out[s] = total.astype(BF16)
            hop(i, s).start()
    wide = dl_ref.shape[3]
    for i, ref in ((0, gate_out), (1, up_out), (2, down_out), (3, down_out)):
        total = local(i, ny - 1)
        hop(i, ny - 2).wait_recv()
        total = total + parts[i][3][ny - 2].astype(F32)
        if i < 2:
            ref[...] = total
        else:
            ref[:, (i - 2) * wide : (i - 1) * wide] = total
    for s in range(ny - 1):
        for i in range(4):
            hop(i, s).wait_send()

    def v_finish(k, c):
        v_copy(k).wait()
        return c

    lax.fori_loop(0, experts - 1, v_finish, 0)
    values = jnp.sum(vr_ref[...], axis=1)
    rank = rank_ref[...]
    back = jnp.zeros(rank.shape, F32)
    for r in range(CAP_OWN + CAP_REP):
        back += jnp.where(rank == float(r), values[:, r : r + 1], 0.0)
    row = lax.broadcasted_iota(jnp.int32, rank.shape, 0)
    for k in range(ids_ref.shape[0]):
        mine = jnp.where(ids_ref[k : k + 1, :] == row, back, 0.0)
        gc_out[k : k + 1, :] = jnp.sum(mine, axis=0, keepdims=True) / prob_ref[k : k + 1, :]


def per_device(tokens, cotangent, expert_ids, gate_probs, home_share, gate_weight, up_weight, down_weight):
    experts = lax.axis_size("expert")
    groups = lax.axis_size("dp")
    nz, ny = experts // NX, groups // 2
    half = experts // 2
    toks, d = tokens.shape
    top = expert_ids.shape[1]
    ff = gate_weight.shape[2]
    wide = d // 2
    share, few = d // groups, ff // groups
    shape = jax.ShapeDtypeStruct

    ids = expert_ids.T
    probs = gate_probs.T.astype(F32)
    cap = jnp.concatenate([home_share + CAP_REP, jnp.full((experts - half,), CAP_OWN, jnp.int32)]).astype(F32)[:, None]
    base, ext, rank = pl.pallas_call(
        pack_kernel,
        out_shape=(shape((experts, 16, d), BF16), shape((half, 8, wide), BF16), shape((experts, toks), F32)),
        in_specs=[VMEM] * 5,
        out_specs=(VMEM,) * 3,
        scratch_shapes=[pltpu.VMEM((experts, toks), F32)],
        name="pack",
    )(ids, probs, cap, tokens, cotangent)

    dma = pltpu.SemaphoreType.DMA
    rb, re = pl.pallas_call(
        functools.partial(send_kernel, nz),
        out_shape=(shape((experts, 16, d), BF16), shape((experts, 8, wide), BF16)),
        in_specs=[ANY] * 2,
        out_specs=(ANY,) * 2,
        scratch_shapes=[dma((experts,)), dma((experts,)), dma((experts,)), dma((experts,)), dma((2,))],
        compiler_params=pltpu.CompilerParams(collective_id=0, has_side_effects=True),
        name="dispatch",
    )(base, ext)

    flag = (lax.axis_index("expert") < half).astype(jnp.int32).reshape(1)
    rows = experts * 10
    gate, up, dl, dr, v = pl.pallas_call(
        expert_kernel,
        out_shape=(
            shape((ny, 2, share, ff), BF16),
            shape((ny, 2, share, ff), BF16),
            shape((ny, 2, few, wide), BF16),
            shape((ny, 2, few, wide), BF16),
            shape((experts, 8, 128), F32),
        ),
        in_specs=[pl.BlockSpec(memory_space=pltpu.SMEM)] + [VMEM] * 5,
        out_specs=(VMEM,) * 5,
        scratch_shapes=[
            pltpu.VMEM((rows, d), BF16),
            pltpu.VMEM((rows, d), BF16),
            pltpu.VMEM((rows, ff), BF16),
            pltpu.VMEM((rows, ff), BF16),
            pltpu.VMEM((rows, ff), BF16),
            pltpu.VMEM((experts, 128), F32),
        ],
        name="expert",
    )(flag, rb, re, gate_weight[0], up_weight[0], down_weight[0])

    gu = (share, ff)
    dn = (few, wide)
    gc, gg, gup, gdn = pl.pallas_call(
        functools.partial(ring_kernel, nz),
        out_shape=(shape((top, toks), F32), shape(gu, F32), shape(gu, F32), shape((few, d), F32)),
        in_specs=[VMEM] * 8,
        out_specs=(VMEM,) * 4,
        scratch_shapes=[pltpu.VMEM((experts, 8, 128), F32)]
        + [pltpu.VMEM((ny,) + s, BF16) for s in (gu, gu, dn, dn)]
        + [pltpu.VMEM((ny - 1,) + s, BF16) for s in (gu, gu, dn, dn)] * 2
        + [dma((experts,)), dma((experts,)), dma((4, ny)), dma((4, ny)), dma((4, ny)), dma((4, ny))],
        compiler_params=pltpu.CompilerParams(collective_id=1, has_side_effects=True),
        name="reduce",
    )(ids, probs, rank, v, gate, up, dl, dr)
    return gc.T, gg[None], gup[None], gdn[None]


def solution(mesh):
    rows = P(("dp", "expert"), None)
    held = P("expert", None, None)
    split = P("expert", "dp", None)
    return jax.shard_map(
        per_device,
        mesh=mesh,
        in_specs=(rows, rows, rows, rows, P(), held, held, held),
        out_specs=(rows, split, split, split),
        check_vma=False,
    )
```

time: 639 us -> 206 us (0.32)
  the two profiles are of different devices: /device:TPU:65 before, /device:TPU:8 now
where the time goes in v1:
time: 206 us
  Pallas kernels  196 us (95%)
  local copies, waits for them, and re-layouts  6.58 us (3%)
    pallas_call x1, Pallas kernels, per_device(): pl.pallas_call(functools.partial(send_kernel, nz), out_shape=(shape((expe...  138 us
    pallas_call x1, Pallas kernels, per_device(): pl.pallas_call(functools.partial(ring_kernel, nz), out_shape=(shape((top,...  42.6 us
    pallas_call x1, Pallas kernels, per_device(): pl.pallas_call(expert_kernel, out_shape=(shape((ny, 2, share, ff), BF16),...  10.4 us
    unnamed x4, local copies, waits for them, and re-layouts  5.87 us
    pallas_call x1, Pallas kernels, per_device(): pl.pallas_call(pack_kernel, out_shape=(shape((experts, 16, d), BF16), sha...  5.25 us

profile of v1, /device:TPU:8, one launch (start us, length us, event | category | flops | bytes accessed | tf_op | source)
XLA Modules:
  0.0 205.5 jit_solution(8749187392559330798)
XLA Ops:
  0.6 0.7 broadcast_add_fusion
  1.3 1.3 convert_bitcast_fusion.prob_ref
  2.6 0.7 copy.12.cap_ref
  3.3 5.2 %pack.1 = (bf16[64,16,1024]{2,1,0:T(8,128)(2,1)}, bf16[32,8,512]{2,1,0:T(8,128)(2,1)}, f32[64,128]{1,0:T(8,128)}) custom-call(s32[4,128]{1,0:T(4,128)} %bitcast.19, f32[4,128]{1,0:T(4,128)} %convert_bitcast_fusion.prob_ref, f32[64,1]{1,0:T(8,128)} %copy.12.cap_ref, bf16[128,1024]{1,0:T(8,128)(2,1)} %tok_ref.1, bf16[128,1024]{1,0:T(8,128)(2,1)} %cot_ref.1), custom_call_target="tpu_custom_call" | custom-call | tf_op jit(solution)/shard_map/pack/pallas_call | solution.py:380
  8.5 138.1 %dispatch.1 = (bf16[64,16,1024]{2,1,0:T(8,128)(2,1)}, bf16[64,8,512]{2,1,0:T(8,128)(2,1)}) custom-call(bf16[64,16,1024]{2,1,0:T(8,128)(2,1)} %get-tuple-element.19.base_ref, bf16[32,8,512]{2,1,0:T(8,128)(2,1)} %get-tuple-element.20.ext_ref), custom_call_target="tpu_custom_call" | custom-call | tf_op jit(solution)/shard_map/dispatch/pallas_call | solution.py:390
  146.6 10.4 %expert.1 = (bf16[8,2,64,384]{3,2,1,0:T(8,128)(2,1)}, bf16[8,2,64,384]{3,2,1,0:T(8,128)(2,1)}, bf16[8,2,24,512]{3,2,1,0:T(8,128)(2,1)}, bf16[8,2,24,512]{3,2,1,0:T(8,128)(2,1)}, f32[64,8,128]{2,1,0:T(8,128)}) custom-call(s32[1]{0:T(128)} %bitcast.3.flag_ref, bf16[64,16,1024]{2,1,0:T(8,128)(2,1)} %get-tuple-element.21.rb_ref, ...), custom_call_target="tpu_custom_call" | custom-call | tf_op jit(solution)/shard_map/expert/pallas_call | solution.py:402
  157.0 42.6 %reduce.1 = (f32[4,128]{1,0:T(4,128)}, f32[64,384]{1,0:T(8,128)}, f32[64,384]{1,0:T(8,128)}, f32[24,1024]{1,0:T(8,128)}) custom-call(s32[4,128]{1,0:T(4,128)} %bitcast.20, f32[4,128]{1,0:T(4,128)} %convert_bitcast_fusion.prob_ref, f32[64,128]{1,0:T(8,128)} %get-tuple-element.18.rank_ref, f32[64,8,128]{2,1,0:T(8,128)} %get-tuple-element.23.v_ref, ...), custom_call_target="tpu_custom_call" | custom-call | tf_op jit(solution)/shard_map/reduce/pallas_call | solution.py:426
  199.7 1.3 copy.17
  200.9 1.5 copy.18
  202.5 1.5 copy.19
  204.0 1.5 copy.20
  (1 shorter events, 0.0 us)

commit v2 on v1

v2 whole, which is shorter than its diff:
```python
import functools

import jax
import jax.numpy as jnp
from jax import lax
from jax.experimental import pallas as pl
from jax.experimental.pallas import tpu as pltpu
from jax.sharding import PartitionSpec as P

MESH = pl.DeviceIdType.MESH
CAP_OWN = 8
CAP_REP = 2
NX = 4
DROPPED = 99.0
F32 = jnp.float32
BF16 = jnp.bfloat16
VMEM = pl.BlockSpec(memory_space=pltpu.VMEM)
ANY = pl.BlockSpec(memory_space=pl.ANY)


def dot(a, b, dims=((1,), (0,))):
    return lax.dot_general(a, b, (dims, ((), ())), preferred_element_type=F32)


def partner(k, nz, zx):
    z, x = zx
    j = k // NX
    odd = j % 2
    dz = nz // 2 + (1 - odd) * (j // 2) - odd * ((j + 1) // 2)
    pz = lax.rem(z + dz + nz, nz)
    px = lax.rem(x + lax.rem(k, NX) + 1, NX)
    return pz, px


def origin(k, nz, zx):
    z, x = zx
    j = k // NX
    odd = j % 2
    dz = nz // 2 + (1 - odd) * (j // 2) - odd * ((j + 1) // 2)
    oz = lax.rem(z - dz + 2 * nz, nz)
    ox = lax.rem(x - lax.rem(k, NX) - 1 + 2 * NX, NX)
    return oz, ox


def layer_kernel(
    nz, ids_ref, prob_ref, home_ref, tok_ref, cot_ref, wg_hbm, wu_hbm, wd_hbm,
    gc_out, gate_out, up_out, down_out,
    rank_ref, pw_ref, base_ref, ext_ref, rb_ref, re_ref,
    wg_ref, wu_ref, wd_ref, x_ref, s_ref, h_ref, pg_ref, pu_ref, v_ref, vr_ref,
    gate_ref, up_ref, dl_ref, dr_ref, peer_g, peer_u, peer_l, peer_r,
    out_g, out_u, out_l, out_r, in_g, in_u, in_l, in_r,
    wsem, bsend, brecv, esend, erecv, vsend, vrecv, dsend, drecv, rsend, rrecv,
):
    me = lax.axis_index("expert")
    zx = (me // NX, lax.rem(me, NX))
    experts = nz * NX
    half = experts // 2
    last = experts - 1
    low = me < half
    dp = lax.axis_index("dp")
    y, core = dp // 2, lax.rem(dp, 2)
    ny = gate_ref.shape[0]
    other = 1 - core
    ahead = lax.rem(y + 1, ny) * 2 + core
    behind = lax.rem(y + ny - 1, ny) * 2 + core
    toks, d = tok_ref.shape
    top = ids_ref.shape[1]
    ff = wg_ref.shape[1]
    wide = d // 2
    barrier = pltpu.get_barrier_semaphore()

    def at_partner(k):
        pz, px = partner(k, nz, zx)
        return pz * NX + px

    def greet(k, c):
        pl.semaphore_signal(barrier, inc=1, device_id={"expert": at_partner(k)}, device_id_type=MESH)
        return c

    lax.fori_loop(0, last, greet, 0)
    for near in (y * 2 + other, ahead, behind):
        pl.semaphore_signal(barrier, inc=1, device_id={"dp": near}, device_id_type=MESH)
    loads = [
        pltpu.make_async_copy(src, dst, wsem.at[i])
        for i, (src, dst) in enumerate(((wg_hbm, wg_ref), (wu_hbm, wu_ref), (wd_hbm, wd_ref)))
    ]
    for load in loads:
        load.start()

    lane = lax.broadcasted_iota(jnp.int32, (toks, experts), 1)
    named = jnp.zeros((toks, experts), F32)
    weight = jnp.zeros((toks, experts), F32)
    for k in range(top):
        hit = ids_ref[:, k : k + 1] == lane
        named += jnp.where(hit, 1.0, 0.0)
        weight += jnp.where(hit, prob_ref[:, k : k + 1].astype(F32), 0.0)
    named, weight = named.astype(BF16), weight.astype(BF16)
    first = lax.broadcasted_iota(jnp.int32, (toks, toks), 0)
    second = lax.broadcasted_iota(jnp.int32, (toks, toks), 1)
    unit = jnp.where(first == second, 1.0, 0.0).astype(BF16)
    earlier = jnp.where(first < second, 1.0, 0.0).astype(BF16)
    turn = ((0,), (0,))
    home = home_ref[...].astype(F32) + CAP_REP
    home_lane = lax.broadcasted_iota(jnp.int32, (experts, half), 1)
    home_row = lax.broadcasted_iota(jnp.int32, (experts, half), 0)
    cap = jnp.sum(jnp.where(home_lane == home_row, home, 0.0), axis=1, keepdims=True)
    cap = jnp.where(lax.broadcasted_iota(jnp.int32, (experts, 1), 0) < half, cap, float(CAP_OWN))
    before = dot(named, earlier, turn)
    kept = (dot(named, unit, turn) > 0.5) & (before < cap)
    rank_ref[...] = jnp.where(kept, before, DROPPED)
    pw_ref[...] = dot(weight, unit, turn)

    group = 8

    @pl.loop(0, experts // group)
    def _(b):
        at = pl.ds(pl.multiple_of(b * group, group), group)
        shape = (group, 16, toks)
        slot = lax.broadcasted_iota(jnp.int32, shape, 1).astype(F32)
        ranks = jnp.broadcast_to(rank_ref[at, :].reshape(group, 1, toks), shape)
        weights = jnp.broadcast_to(pw_ref[at, :].reshape(group, 1, toks), shape)
        pick = jnp.where((ranks == slot) & (slot < 7.5), 1.0, 0.0).reshape(group * 16, toks).astype(BF16)
        scale = jnp.where(ranks == slot - 8.0, weights, 0.0).reshape(group * 16, toks).astype(BF16)
        rows = dot(pick, tok_ref[...]) + dot(scale, cot_ref[...])
        base_ref[at] = rows.reshape(group, 16, d).astype(BF16)

    big = 16 if half % 16 == 0 else half

    @pl.loop(0, half // big)
    def _(b):
        at = pl.ds(pl.multiple_of(b * big, big), big)
        shape = (big, 8, toks)
        place = lax.broadcasted_iota(jnp.int32, shape, 1)
        ranks = jnp.broadcast_to(rank_ref[at, :].reshape(big, 1, toks), shape)
        weights = jnp.broadcast_to(pw_ref[at, :].reshape(big, 1, toks), shape)
        here = ranks == (8 + place % 2).astype(F32)
        total = jnp.zeros((big * 8, wide), F32)
        for q in range(2):
            pick = jnp.where(here & (place // 2 == 2 * q), 1.0, 0.0).reshape(big * 8, toks).astype(BF16)
            scale = jnp.where(here & (place // 2 == 2 * q + 1), weights, 0.0).reshape(big * 8, toks).astype(BF16)
            cols = slice(q * wide, (q + 1) * wide)
            total += dot(pick, tok_ref[:, cols]) + dot(scale, cot_ref[:, cols])
        ext_ref[at] = total.reshape(big, 8, wide).astype(BF16)

    pl.semaphore_wait(barrier, last + 3)

    def base_copy(k, peer):
        return pltpu.make_async_remote_copy(
            src_ref=base_ref.at[peer],
            dst_ref=rb_ref.at[k],
            send_sem=bsend.at[k],
            recv_sem=brecv.at[k],
            device_id={"expert": peer},
            device_id_type=MESH,
        )

    def ext_copy(k, peer):
        return pltpu.make_async_remote_copy(
            src_ref=ext_ref.at[peer],
            dst_ref=re_ref.at[k],
            send_sem=esend.at[k],
            recv_sem=erecv.at[k],
            device_id={"expert": peer},
            device_id_type=MESH,
        )

    def issue(k, c):
        peer = at_partner(k)
        base_copy(k, peer).start()

        @pl.when(peer < half)
        def _():
            ext_copy(k, peer).start()

        return c

    lax.fori_loop(0, last, issue, 0)
    rb_ref[last] = base_ref[me]

    @pl.when(low)
    def _():
        re_ref[last] = ext_ref[me]

    for load in loads:
        load.wait()

    many = 16
    rows = many * 10

    def v_copy(k):
        oz, ox = origin(k, nz, zx)
        return pltpu.make_async_remote_copy(
            src_ref=v_ref.at[k],
            dst_ref=vr_ref.at[me],
            send_sem=vsend.at[k],
            recv_sem=vrecv.at[k],
            device_id={"expert": oz * NX + ox},
            device_id_type=MESH,
        )

    def v_issue(k, c):
        v_copy(k).start()
        return c

    def on_group(g, c):
        def arrive(i, c2):
            k = g * many + i

            @pl.when(k < last)
            def _():
                base_copy(k, me).wait_recv()

            @pl.when((k < last) & low)
            def _():
                ext_copy(k, 0).wait_recv()

            return c2

        lax.fori_loop(0, many, arrive, 0)
        src = pl.ds(pl.multiple_of(g * many, many), many)
        at = pl.multiple_of(g * rows, 32)
        part = rb_ref[src].astype(F32)
        x_ref[pl.ds(at, many * 8), :] = part[:, :8, :].reshape(many * 8, d).astype(BF16)
        s_ref[pl.ds(at, many * 8), :] = part[:, 8:, :].reshape(many * 8, d).astype(BF16)
        extra = re_ref[src].astype(F32).reshape(many * 8, wide)
        extra = jnp.where(low, extra, 0.0).astype(BF16)
        out_row = lax.broadcasted_iota(jnp.int32, (4 * many, many * 8), 0)
        in_row = lax.broadcasted_iota(jnp.int32, (4 * many, many * 8), 1)
        wanted = (out_row % many) * 8 + out_row // many
        for q in range(2):
            pick = jnp.where(in_row == wanted + 4 * q, 1.0, 0.0).astype(BF16)
            both = dot(pick, extra).astype(BF16)
            cols = slice(q * wide, (q + 1) * wide)
            x_ref[pl.ds(at + many * 8, many * 2), cols] = both[: 2 * many]
            s_ref[pl.ds(at + many * 8, many * 2), cols] = both[2 * many :]
        here = pl.ds(at, rows)
        x, s = x_ref[here, :], s_ref[here, :]
        a = dot(x, wg_ref[...])
        b = dot(x, wu_ref[...])
        sig = jax.nn.sigmoid(a)
        silu = a * sig
        hidden = (silu * b).astype(BF16)
        h_ref[here, :] = hidden
        cot = dot(s, wd_ref[...], ((1,), (1,)))
        pg_ref[here, :] = (cot * b * sig * (1.0 + a * (1.0 - sig))).astype(BF16)
        pu_ref[here, :] = (cot * silu).astype(BF16)
        out = dot(hidden, wd_ref[...])
        col = jnp.sum(out * s.astype(F32), axis=1, keepdims=True)
        own = lax.broadcasted_iota(jnp.int32, (many * 8, 128), 1)
        sub = lax.broadcasted_iota(jnp.int32, (many * 8, 128), 0) % 8
        tile = jnp.sum(jnp.where(own == sub, col[: many * 8], 0.0).reshape(many, 8, 128), axis=1)
        own = lax.broadcasted_iota(jnp.int32, (many, 128), 1)
        for j in range(2):
            tile += jnp.where(own == 8 + j, col[many * (8 + j) : many * (9 + j)], 0.0)
        v_ref[src] = tile.reshape(many, 1, 128)
        return c

    groups = experts // many

    def do_group(g, c):
        on_group(g, c)
        lax.fori_loop(g * many, g * many + many, v_issue, 0)
        return c

    lax.fori_loop(0, groups - 1, do_group, 0)
    on_group(groups - 1, 0)

    parts = (
        (gate_ref, peer_g, out_g, in_g, 1),
        (up_ref, peer_u, out_u, in_u, -1),
        (dl_ref, peer_l, out_l, in_l, 1),
        (dr_ref, peer_r, out_r, in_r, -1),
    )

    def owner(way, s):
        return lax.rem(y - way * (1 + s) + 2 * ny, ny)

    def across(i, s):
        src, dst, _, _, way = parts[i]
        o = owner(way, s)
        return pltpu.make_async_remote_copy(
            src_ref=src.at[o, other],
            dst_ref=dst.at[o],
            send_sem=dsend.at[i, s],
            recv_sem=drecv.at[i, s],
            device_id={"dp": y * 2 + other},
            device_id_type=MESH,
        )

    def hop(i, s):
        _, _, out, inn, way = parts[i]
        return pltpu.make_async_remote_copy(
            src_ref=out.at[s],
            dst_ref=inn.at[s],
            send_sem=rsend.at[i, s],
            recv_sem=rrecv.at[i, s],
            device_id={"dp": ahead if way == 1 else behind},
            device_id_type=MESH,
        )

    share, few = gate_ref.shape[2], dl_ref.shape[2]

    def product(i, s):
        ref, way, pre = ((gate_ref, 1, pg_ref), (up_ref, -1, pu_ref))[i]
        o = owner(way, s)
        xs = x_ref[:, pl.ds(pl.multiple_of(o * 2 * share, 2 * share), 2 * share)]
        ref[o] = dot(xs, pre[...], turn).reshape(2, share, ff).astype(BF16)

    def local(i, s):
        src, dst, _, _, way = parts[i]
        o = owner(way, s)
        across(i, s).wait()
        return src[o, core].astype(F32) + dst[o].astype(F32)

    def ring(s):
        for i in range(4):
            _, _, out, inn, _ = parts[i]
            total = local(i, s)
            if s > 0:
                hop(i, s - 1).wait_recv()
                total = total + inn[s - 1].astype(F32)
            out[s] = total.astype(BF16)
            hop(i, s).start()

    product(0, 0)
    product(1, 0)
    for ref, at in ((dl_ref, 0), (dr_ref, wide)):
        down = dot(h_ref[...], s_ref[:, at : at + wide], turn)
        ref[...] = down.reshape(ny, 2, few, wide).astype(BF16)
    for i in range(2):
        across(i, 0).start()
    for s in range(ny):
        for i in range(2, 4):
            across(i, s).start()
    lax.fori_loop(last - many + 1, last, v_issue, 0)
    vr_ref[me] = v_ref[last]
    for s in range(1, ny):
        product(0, s)
        product(1, s)
        for i in range(2):
            across(i, s).start()
        if s >= 2:
            ring(s - 2)
    ring(ny - 2)

    def v_finish(k, c):
        v_copy(k).wait()
        return c

    lax.fori_loop(0, last, v_finish, 0)
    values = jnp.transpose(vr_ref[...].reshape(experts, 128))
    place = dot(jnp.where(second < first, 1.0, 0.0).astype(BF16), named)
    back = jnp.zeros((toks, experts), F32)
    for r in range(CAP_OWN + CAP_REP):
        back += jnp.where(place == float(r), values[r : r + 1, :], 0.0)
    home = jnp.concatenate([home, jnp.full((1, experts - half), float(CAP_OWN), F32)], axis=1)
    back = jnp.where(place < home, back, 0.0)
    for k in range(top):
        mine = jnp.where(ids_ref[:, k : k + 1] == lane, back, 0.0)
        gc_out[:, k : k + 1] = jnp.sum(mine, axis=1, keepdims=True) / prob_ref[:, k : k + 1].astype(F32)

    for i, ref in ((0, gate_out), (1, up_out), (2, down_out), (3, down_out)):
        total = local(i, ny - 1)
        hop(i, ny - 2).wait_recv()
        total = total + parts[i][3][ny - 2].astype(F32)
        if i < 2:
            ref[...] = total
        else:
            ref[:, (i - 2) * wide : (i - 1) * wide] = total
    for s in range(ny - 1):
        for i in range(4):
            hop(i, s).wait_send()

    def sent(k, c):
        base_copy(k, me).wait_send()

        @pl.when(at_partner(k) < half)
        def _():
            ext_copy(k, 0).wait_send()

        return c

    lax.fori_loop(0, last, sent, 0)


def pass_kernel(*refs):
    n = len(refs) // 2
    for src, dst in zip(refs[:n], refs[n:]):
        dst[...] = src[...]


def per_device(tokens, cotangent, expert_ids, gate_probs, home_share, gate_weight, up_weight, down_weight):
    experts = lax.axis_size("expert")
    groups = lax.axis_size("dp")
    nz, ny = experts // NX, groups // 2
    half = experts // 2
    toks, d = tokens.shape
    top = expert_ids.shape[1]
    ff = gate_weight.shape[2]
    wide = d // 2
    share, few = d // groups, ff // groups
    shape = jax.ShapeDtypeStruct
    dma = pltpu.SemaphoreType.DMA
    rows = experts * 10
    gu = (share, ff)
    dn = (few, wide)
    outs = (shape((toks, top), F32), shape(gu, F32), shape(gu, F32), shape((few, d), F32))

    def held(*dims, dtype=BF16):
        return pltpu.VMEM(dims, dtype)

    raw = pl.pallas_call(
        functools.partial(layer_kernel, nz),
        out_shape=outs,
        in_specs=[VMEM] * 5 + [ANY] * 3,
        out_specs=(VMEM,) * 4,
        scratch_shapes=[
            held(experts, toks, dtype=F32),
            held(experts, toks, dtype=F32),
            held(experts, 16, d),
            held(half, 8, wide),
            held(experts, 16, d),
            held(experts, 8, wide),
            held(d, ff),
            held(d, ff),
            held(ff, d),
            held(rows, d),
            held(rows, d),
            held(rows, ff),
            held(rows, ff),
            held(rows, ff),
            held(experts, 1, 128, dtype=F32),
            held(experts, 1, 128, dtype=F32),
        ]
        + [held(ny, 2, *s) for s in (gu, gu, dn, dn)]
        + [held(ny, *s) for s in (gu, gu, dn, dn)]
        + [held(ny - 1, *s) for s in (gu, gu, dn, dn)] * 2
        + [dma((3,))]
        + [dma((experts,))] * 6
        + [dma((4, ny))] * 4,
        compiler_params=pltpu.CompilerParams(collective_id=0, has_side_effects=True),
        name="layer",
    )(expert_ids, gate_probs, home_share[None], tokens, cotangent, gate_weight[0], up_weight[0], down_weight[0])
    gc, gg, gup, gdn = pl.pallas_call(
        pass_kernel, out_shape=outs, in_specs=[VMEM] * 4, out_specs=(VMEM,) * 4, name="hand_on"
    )(*raw)
    return gc, gg[None], gup[None], gdn[None]


def solution(mesh):
    rows = P(("dp", "expert"), None)
    held = P("expert", None, None)
    split = P("expert", "dp", None)
    return jax.shard_map(
        per_device,
        mesh=mesh,
        in_specs=(rows, rows, rows, rows, P(), held, held, held),
        out_specs=(rows, split, split, split),
        check_vma=False,
    )
```

time: 206 us -> 182 us (0.88)
  the two profiles are of different devices: /device:TPU:8 before, /device:TPU:2 now
where the time goes in v2:
time: 182 us
  Pallas kernels  177 us (97%)
  local copies, waits for them, and re-layouts  3.64 us (2%)
    pallas_call x1, Pallas kernels, per_device(): pl.pallas_call(functools.partial(layer_kernel, nz), out_shape=outs, in_sp...  175 us

profile of v2, /device:TPU:2, one launch (start us, length us, event | category | flops | bytes accessed | tf_op | source)
XLA Modules:
  0.0 181.5 jit_solution(110316088940954437)
XLA Ops:
  0.6 0.0 copy-start.1
  0.6 0.7 copy-done.1
  1.3 0.0 copy-start
  1.3 0.7 copy.13.prob_ref
  2.0 0.0 copy-done
  2.0 0.7 copy.12.ids_ref
  2.8 175.5 %layer.1 = (f32[128,4]{1,0:T(8,128)}, f32[64,384]{1,0:T(8,128)}, f32[64,384]{1,0:T(8,128)}, f32[24,1024]{1,0:T(8,128)}) custom-call(s32[128,4]{1,0:T(8,128)} %copy.12.ids_ref, bf16[128,4]{1,0:T(8,128)(2,1)} %copy.13.prob_ref, s32[1,32]{1,0:T(1,128)} %bitcast.10, bf16[128,1024]{1,0:T(8,128)(2,1)} %tok_ref.1, bf16[128,1024]{1,0:T(8,128)(2,1)} %cot_ref.1, ...), custom_call_target="tpu_custom_call" | custom-call | tf_op jit(solution)/shard_map/layer/pallas_call | solution.py:412
  178.3 1.8 hand_on.1
  180.0 1.5 copy.14
Async XLA Ops:
  0.6 0.7 copy-start.1
  1.3 0.7 copy-start

commit v3 on v2

--- a/solution.py
+++ b/solution.py
@@ -64,7 +64,7 @@
     ahead = lax.rem(y + 1, ny) * 2 + core
     behind = lax.rem(y + ny - 1, ny) * 2 + core
     toks, d = tok_ref.shape
-    top = ids_ref.shape[1]
+    top = ids_ref.shape[0]
     ff = wg_ref.shape[1]
     wide = d // 2
     barrier = pltpu.get_barrier_semaphore()
@@ -87,28 +87,27 @@
     for load in loads:
         load.start()
 
-    lane = lax.broadcasted_iota(jnp.int32, (toks, experts), 1)
-    named = jnp.zeros((toks, experts), F32)
-    weight = jnp.zeros((toks, experts), F32)
+    turn = ((0,), (0,))
+    row = lax.broadcasted_iota(jnp.int32, (experts, toks), 0)
+    probs = prob_ref[...].astype(F32)
+    named = jnp.zeros((experts, toks), F32)
+    weight = jnp.zeros((experts, toks), F32)
     for k in range(top):
-        hit = ids_ref[:, k : k + 1] == lane
+        hit = ids_ref[k : k + 1, :] == row
         named += jnp.where(hit, 1.0, 0.0)
-        weight += jnp.where(hit, prob_ref[:, k : k + 1].astype(F32), 0.0)
-    named, weight = named.astype(BF16), weight.astype(BF16)
+        weight += jnp.where(hit, probs[k : k + 1, :], 0.0)
     first = lax.broadcasted_iota(jnp.int32, (toks, toks), 0)
     second = lax.broadcasted_iota(jnp.int32, (toks, toks), 1)
-    unit = jnp.where(first == second, 1.0, 0.0).astype(BF16)
     earlier = jnp.where(first < second, 1.0, 0.0).astype(BF16)
-    turn = ((0,), (0,))
     home = home_ref[...].astype(F32) + CAP_REP
     home_lane = lax.broadcasted_iota(jnp.int32, (experts, half), 1)
     home_row = lax.broadcasted_iota(jnp.int32, (experts, half), 0)
     cap = jnp.sum(jnp.where(home_lane == home_row, home, 0.0), axis=1, keepdims=True)
     cap = jnp.where(lax.broadcasted_iota(jnp.int32, (experts, 1), 0) < half, cap, float(CAP_OWN))
-    before = dot(named, earlier, turn)
-    kept = (dot(named, unit, turn) > 0.5) & (before < cap)
+    before = dot(named.astype(BF16), earlier)
+    kept = (named > 0.5) & (before < cap)
     rank_ref[...] = jnp.where(kept, before, DROPPED)
-    pw_ref[...] = dot(weight, unit, turn)
+    pw_ref[...] = weight
 
     group = 8
 
@@ -265,111 +264,128 @@
     lax.fori_loop(0, groups - 1, do_group, 0)
     on_group(groups - 1, 0)
 
+    far = ny // 2
     parts = (
-        (gate_ref, peer_g, out_g, in_g, 1),
-        (up_ref, peer_u, out_u, in_u, -1),
-        (dl_ref, peer_l, out_l, in_l, 1),
-        (dr_ref, peer_r, out_r, in_r, -1),
+        (gate_ref, peer_g, out_g, in_g),
+        (up_ref, peer_u, out_u, in_u),
+        (dl_ref, peer_l, out_l, in_l),
+        (dr_ref, peer_r, out_r, in_r),
     )
-
-    def owner(way, s):
-        return lax.rem(y - way * (1 + s) + 2 * ny, ny)
-
-    def across(i, s):
-        src, dst, _, _, way = parts[i]
-        o = owner(way, s)
+    ways = (1, -1)
+
+    def length(i, w):
+        return far if (i % 2 == 0) == (w == 0) else ny - 1 - far
+
+    def chip(off):
+        return lax.rem(y + off + ny, ny)
+
+    def across(i, off):
+        src, dst, _, _ = parts[i]
+        o = chip(off)
         return pltpu.make_async_remote_copy(
             src_ref=src.at[o, other],
             dst_ref=dst.at[o],
-            send_sem=dsend.at[i, s],
-            recv_sem=drecv.at[i, s],
+            send_sem=dsend.at[i, off % ny],
+            recv_sem=drecv.at[i, off % ny],
             device_id={"dp": y * 2 + other},
             device_id_type=MESH,
         )
 
-    def hop(i, s):
-        _, _, out, inn, way = parts[i]
+    def hop(i, w, t):
+        _, _, out, inn = parts[i]
+        at = w * far + t
         return pltpu.make_async_remote_copy(
-            src_ref=out.at[s],
-            dst_ref=inn.at[s],
-            send_sem=rsend.at[i, s],
-            recv_sem=rrecv.at[i, s],
-            device_id={"dp": ahead if way == 1 else behind},
+            src_ref=out.at[at],
+            dst_ref=inn.at[at],
+            send_sem=rsend.at[i, at],
+            recv_sem=rrecv.at[i, at],
+            device_id={"dp": ahead if w == 0 else behind},
             device_id_type=MESH,
         )
 
     share, few = gate_ref.shape[2], dl_ref.shape[2]
 
-    def product(i, s):
-        ref, way, pre = ((gate_ref, 1, pg_ref), (up_ref, -1, pu_ref))[i]
-        o = owner(way, s)
+    def product(off):
+        o = chip(off)
         xs = x_ref[:, pl.ds(pl.multiple_of(o * 2 * share, 2 * share), 2 * share)]
-        ref[o] = dot(xs, pre[...], turn).reshape(2, share, ff).astype(BF16)
-
-    def local(i, s):
-        src, dst, _, _, way = parts[i]
-        o = owner(way, s)
-        across(i, s).wait()
+        gate_ref[o] = dot(xs, pg_ref[...], turn).reshape(2, share, ff).astype(BF16)
+        up_ref[o] = dot(xs, pu_ref[...], turn).reshape(2, share, ff).astype(BF16)
+
+    def cross(off, which):
+        for i in which:
+            across(i, off).start()
+
+    joined = set()
+
+    def local(i, off):
+        if (i, off % ny) not in joined:
+            joined.add((i, off % ny))
+            across(i, off).wait()
+        src, dst, _, _ = parts[i]
+        o = chip(off)
         return src[o, core].astype(F32) + dst[o].astype(F32)
 
-    def ring(s):
-        for i in range(4):
-            _, _, out, inn, _ = parts[i]
-            total = local(i, s)
-            if s > 0:
-                hop(i, s - 1).wait_recv()
-                total = total + inn[s - 1].astype(F32)
-            out[s] = total.astype(BF16)
-            hop(i, s).start()
-
-    product(0, 0)
-    product(1, 0)
+    def ring(t):
+        chains = [(i, w) for i in range(4) for w in range(2)]
+        chains.sort(key=lambda c: -length(*c))
+        for i, w in chains:
+            if t < length(i, w):
+                total = local(i, ways[w] * (length(i, w) - t))
+                if t > 0:
+                    hop(i, w, t - 1).wait_recv()
+                    total = total + parts[i][3][w * far + t - 1].astype(F32)
+                parts[i][2][w * far + t] = total.astype(BF16)
+                hop(i, w, t).start()
+
+    steps = [far]
+    for m in range(far - 1, 0, -1):
+        steps += [m, -m]
+    steps += [0]
+    product(far)
     for ref, at in ((dl_ref, 0), (dr_ref, wide)):
         down = dot(h_ref[...], s_ref[:, at : at + wide], turn)
         ref[...] = down.reshape(ny, 2, few, wide).astype(BF16)
-    for i in range(2):
-        across(i, 0).start()
-    for s in range(ny):
-        for i in range(2, 4):
-            across(i, s).start()
+    cross(far, range(4))
     lax.fori_loop(last - many + 1, last, v_issue, 0)
     vr_ref[me] = v_ref[last]
-    for s in range(1, ny):
-        product(0, s)
-        product(1, s)
-        for i in range(2):
-            across(i, s).start()
-        if s >= 2:
-            ring(s - 2)
-    ring(ny - 2)
+    t = 0
+    for n, off in enumerate(steps[1:]):
+        product(off)
+        cross(off, range(4))
+        if n % 2 == 1:
+            ring(t)
+            t += 1
+    for rest in range(t, far):
+        ring(rest)
 
     def v_finish(k, c):
         v_copy(k).wait()
         return c
 
     lax.fori_loop(0, last, v_finish, 0)
-    values = jnp.transpose(vr_ref[...].reshape(experts, 128))
-    place = dot(jnp.where(second < first, 1.0, 0.0).astype(BF16), named)
-    back = jnp.zeros((toks, experts), F32)
+    values = vr_ref[...].reshape(experts, 128)
+    place = rank_ref[...]
+    back = jnp.zeros((experts, toks), F32)
     for r in range(CAP_OWN + CAP_REP):
-        back += jnp.where(place == float(r), values[r : r + 1, :], 0.0)
-    home = jnp.concatenate([home, jnp.full((1, experts - half), float(CAP_OWN), F32)], axis=1)
-    back = jnp.where(place < home, back, 0.0)
+        back += jnp.where(place == float(r), values[:, r : r + 1], 0.0)
     for k in range(top):
-        mine = jnp.where(ids_ref[:, k : k + 1] == lane, back, 0.0)
-        gc_out[:, k : k + 1] = jnp.sum(mine, axis=1, keepdims=True) / prob_ref[:, k : k + 1].astype(F32)
+        mine = jnp.where(ids_ref[k : k + 1, :] == row, back, 0.0)
+        gc_out[k : k + 1, :] = jnp.sum(mine, axis=0, keepdims=True) / probs[k : k + 1, :]
 
     for i, ref in ((0, gate_out), (1, up_out), (2, down_out), (3, down_out)):
-        total = local(i, ny - 1)
-        hop(i, ny - 2).wait_recv()
-        total = total + parts[i][3][ny - 2].astype(F32)
+        total = local(i, 0)
+        for w in range(2):
+            if length(i, w) > 0:
+                hop(i, w, length(i, w) - 1).wait_recv()
+                total = total + parts[i][3][w * far + length(i, w) - 1].astype(F32)
         if i < 2:
             ref[...] = total
         else:
             ref[:, (i - 2) * wide : (i - 1) * wide] = total
-    for s in range(ny - 1):
-        for i in range(4):
-            hop(i, s).wait_send()
+    for i in range(4):
+        for w in range(2):
+            for t in range(length(i, w)):
+                hop(i, w, t).wait_send()
 
     def sent(k, c):
         base_copy(k, me).wait_send()
@@ -404,7 +420,7 @@
     rows = experts * 10
     gu = (share, ff)
     dn = (few, wide)
-    outs = (shape((toks, top), F32), shape(gu, F32), shape(gu, F32), shape((few, d), F32))
+    outs = (shape((top, toks), F32), shape(gu, F32), shape(gu, F32), shape((few, d), F32))
 
     def held(*dims, dtype=BF16):
         return pltpu.VMEM(dims, dtype)
@@ -434,17 +450,17 @@
         ]
         + [held(ny, 2, *s) for s in (gu, gu, dn, dn)]
         + [held(ny, *s) for s in (gu, gu, dn, dn)]
-        + [held(ny - 1, *s) for s in (gu, gu, dn, dn)] * 2
+        + [held(ny, *s) for s in (gu, gu, dn, dn)] * 2
         + [dma((3,))]
         + [dma((experts,))] * 6
         + [dma((4, ny))] * 4,
         compiler_params=pltpu.CompilerParams(collective_id=0, has_side_effects=True),
         name="layer",
-    )(expert_ids, gate_probs, home_share[None], tokens, cotangent, gate_weight[0], up_weight[0], down_weight[0])
+    )(expert_ids.T, gate_probs.T, home_share[None], tokens, cotangent, gate_weight[0], up_weight[0], down_weight[0])
     gc, gg, gup, gdn = pl.pallas_call(
         pass_kernel, out_shape=outs, in_specs=[VMEM] * 4, out_specs=(VMEM,) * 4, name="hand_on"
     )(*raw)
-    return gc, gg[None], gup[None], gdn[None]
+    return gc.T, gg[None], gup[None], gdn[None]
 
 
 def solution(mesh):

time: 182 us -> 168 us (0.923)
  Pallas kernels: 177 us -> 167 us
  local copies, waits for them, and re-layouts: 3.64 us -> 0 us
    pallas_call x1, Pallas kernels: 175 us -> 165 us  [per_device(): pl.pallas_call(functools.partial(layer_kernel, nz), out_shape=outs, in_sp...]
    unnamed x7 -> x0, local copies, waits for them, and re-layouts: 3.64 us -> none
where the time goes in v3:
time: 168 us
  Pallas kernels  167 us (99%)
    pallas_call x1, Pallas kernels, per_device(): pl.pallas_call(functools.partial(layer_kernel, nz), out_shape=outs, in_sp...  165 us

profile of v3, /device:TPU:2, one launch (start us, length us, event | category | flops | bytes accessed | tf_op | source)
XLA Modules:
  0.0 167.6 jit_solution(688994851165002490)
XLA Ops:
  0.6 165.3 %layer.1 = (f32[4,128]{1,0:T(4,128)}, f32[64,384]{1,0:T(8,128)}, f32[64,384]{1,0:T(8,128)}, f32[24,1024]{1,0:T(8,128)}) custom-call(s32[4,128]{1,0:T(4,128)} %bitcast.13, bf16[4,128]{1,0:T(4,128)(2,1)} %bitcast.14, s32[1,32]{1,0:T(1,128)} %bitcast.15, bf16[128,1024]{1,0:T(8,128)(2,1)} %tok_ref.1, bf16[128,1024]{1,0:T(8,128)(2,1)} %cot_ref.1, ...), custom_call_target="tpu_custom_call" | custom-call | tf_op jit(solution)/shard_map/layer/pallas_call | solution.py:428
  165.9 1.7 %hand_on.1 = (f32[4,128]{1,0:T(4,128)}, f32[64,384]{1,0:T(8,128)}, f32[64,384]{1,0:T(8,128)}, f32[24,1024]{1,0:T(8,128)}) custom-call(f32[4,128]{1,0:T(4,128)} %get-tuple-element.12.refs_0_, f32[64,384]{1,0:T(8,128)} %get-tuple-element.13.refs_1_, f32[64,384]{1,0:T(8,128)} %get-tuple-element.14.refs_2_, f32[24,1024]{1,0:T(8,128)} %get-tuple-element.15.refs_3_), custom_call_target="tpu_custom_call" | custom-call | tf_op jit(solution)/shard_map/hand_on/pallas_call | solution.py:460

commit v4 on v3

--- a/solution.py
+++ b/solution.py
@@ -32,24 +32,26 @@
     return pz, px
 
 
+def toward(b):
+    odd = b % 2
+    return odd * ((b + 1) // 2) - (1 - odd) * (b // 2)
+
+
 def origin(k, nz, zx):
     z, x = zx
-    j = k // NX
-    odd = j % 2
-    dz = nz // 2 + (1 - odd) * (j // 2) - odd * ((j + 1) // 2)
-    oz = lax.rem(z - dz + 2 * nz, nz)
-    ox = lax.rem(x - lax.rem(k, NX) - 1 + 2 * NX, NX)
+    oz = lax.rem(z - toward(k // NX) + 2 * nz, nz)
+    ox = lax.rem(x - lax.rem(k, NX) + NX, NX)
     return oz, ox
 
 
 def layer_kernel(
     nz, ids_ref, prob_ref, home_ref, tok_ref, cot_ref, wg_hbm, wu_hbm, wd_hbm,
     gc_out, gate_out, up_out, down_out,
-    rank_ref, pw_ref, base_ref, ext_ref, rb_ref, re_ref,
+    rank_ref, seen_ref, seen_pw_ref, meta_ref, blk_ref, base_ref, ext_ref, rb_ref, re_ref,
     wg_ref, wu_ref, wd_ref, x_ref, s_ref, h_ref, pg_ref, pu_ref, v_ref, vr_ref,
     gate_ref, up_ref, dl_ref, dr_ref, peer_g, peer_u, peer_l, peer_r,
     out_g, out_u, out_l, out_r, in_g, in_u, in_l, in_r,
-    wsem, bsend, brecv, esend, erecv, vsend, vrecv, dsend, drecv, rsend, rrecv,
+    wsem, bsend, brecv, esend, erecv, vsend, vrecv, msend, mrecv, gsend, grecv, dsend, drecv, rsend, rrecv,
 ):
     me = lax.axis_index("expert")
     zx = (me // NX, lax.rem(me, NX))
@@ -91,11 +93,9 @@
     row = lax.broadcasted_iota(jnp.int32, (experts, toks), 0)
     probs = prob_ref[...].astype(F32)
     named = jnp.zeros((experts, toks), F32)
-    weight = jnp.zeros((experts, toks), F32)
     for k in range(top):
-        hit = ids_ref[k : k + 1, :] == row
-        named += jnp.where(hit, 1.0, 0.0)
-        weight += jnp.where(hit, probs[k : k + 1, :], 0.0)
+        named += jnp.where(ids_ref[k : k + 1, :] == row, 1.0, 0.0)
+    meta_ref[0] = jnp.concatenate([ids_ref[...].astype(F32), probs], axis=0)
     first = lax.broadcasted_iota(jnp.int32, (toks, toks), 0)
     second = lax.broadcasted_iota(jnp.int32, (toks, toks), 1)
     earlier = jnp.where(first < second, 1.0, 0.0).astype(BF16)
@@ -107,78 +107,117 @@
     before = dot(named.astype(BF16), earlier)
     kept = (named > 0.5) & (before < cap)
     rank_ref[...] = jnp.where(kept, before, DROPPED)
-    pw_ref[...] = weight
-
-    group = 8
-
-    @pl.loop(0, experts // group)
-    def _(b):
-        at = pl.ds(pl.multiple_of(b * group, group), group)
-        shape = (group, 16, toks)
-        slot = lax.broadcasted_iota(jnp.int32, shape, 1).astype(F32)
-        ranks = jnp.broadcast_to(rank_ref[at, :].reshape(group, 1, toks), shape)
-        weights = jnp.broadcast_to(pw_ref[at, :].reshape(group, 1, toks), shape)
-        pick = jnp.where((ranks == slot) & (slot < 7.5), 1.0, 0.0).reshape(group * 16, toks).astype(BF16)
-        scale = jnp.where(ranks == slot - 8.0, weights, 0.0).reshape(group * 16, toks).astype(BF16)
-        rows = dot(pick, tok_ref[...]) + dot(scale, cot_ref[...])
-        base_ref[at] = rows.reshape(group, 16, d).astype(BF16)
-
-    big = 16 if half % 16 == 0 else half
-
-    @pl.loop(0, half // big)
-    def _(b):
-        at = pl.ds(pl.multiple_of(b * big, big), big)
-        shape = (big, 8, toks)
-        place = lax.broadcasted_iota(jnp.int32, shape, 1)
-        ranks = jnp.broadcast_to(rank_ref[at, :].reshape(big, 1, toks), shape)
-        weights = jnp.broadcast_to(pw_ref[at, :].reshape(big, 1, toks), shape)
-        here = ranks == (8 + place % 2).astype(F32)
-        total = jnp.zeros((big * 8, wide), F32)
-        for q in range(2):
-            pick = jnp.where(here & (place // 2 == 2 * q), 1.0, 0.0).reshape(big * 8, toks).astype(BF16)
-            scale = jnp.where(here & (place // 2 == 2 * q + 1), weights, 0.0).reshape(big * 8, toks).astype(BF16)
-            cols = slice(q * wide, (q + 1) * wide)
-            total += dot(pick, tok_ref[:, cols]) + dot(scale, cot_ref[:, cols])
-        ext_ref[at] = total.reshape(big, 8, wide).astype(BF16)
+
+    plane = zx[0] * NX
+    eight = lax.broadcasted_iota(jnp.int32, (8, toks), 0) + plane
+    held_lane = lax.broadcasted_iota(jnp.int32, (8, half), 1)
+    held_row = lax.broadcasted_iota(jnp.int32, (8, half), 0) + plane
+    room = jnp.sum(jnp.where(held_lane == held_row, home, 0.0), axis=1, keepdims=True)
+    room = jnp.where(low, room, float(CAP_OWN))
 
     pl.semaphore_wait(barrier, last + 3)
 
-    def base_copy(k, peer):
+    mid = nz // 2
+
+    def meta_copy(n):
+        pz = lax.rem(zx[0] + toward(n) + nz, nz)
         return pltpu.make_async_remote_copy(
-            src_ref=base_ref.at[peer],
-            dst_ref=rb_ref.at[k],
-            send_sem=bsend.at[k],
-            recv_sem=brecv.at[k],
+            src_ref=meta_ref.at[0],
+            dst_ref=meta_ref.at[n],
+            send_sem=msend.at[n],
+            recv_sem=mrecv.at[n],
+            device_id={"expert": pz * NX + zx[1]},
+            device_id_type=MESH,
+        )
+
+    def block_hop(c, t, source=None):
+        half_of, back = c % 2, c // 2
+        if source is None:
+            source = blk_ref.at[2 * t - 3 + back, half_of]
+        pz = lax.rem(zx[0] + (nz - 1 if back else 1), nz)
+        return pltpu.make_async_remote_copy(
+            src_ref=source,
+            dst_ref=blk_ref.at[2 * t - t // mid if back else 2 * t - 1, half_of],
+            send_sem=gsend.at[c, t],
+            recv_sem=grecv.at[c, t],
+            device_id={"expert": pz * NX + zx[1]},
+            device_id_type=MESH,
+        )
+
+    def meta_issue(n, c):
+        meta_copy(n).start()
+        return c
+
+    for c in (0, 3, 1, 2):
+        block_hop(c, 1, (tok_ref, cot_ref)[c % 2]).start()
+    lax.fori_loop(1, nz, meta_issue, 0)
+
+    def side_copy(src, dst, send, recv, k):
+        peer = plane + lax.rem(zx[1] + lax.rem(k, NX), NX)
+        return pltpu.make_async_remote_copy(
+            src_ref=src.at[k],
+            dst_ref=dst.at[k],
+            send_sem=send.at[k],
+            recv_sem=recv.at[k],
             device_id={"expert": peer},
             device_id_type=MESH,
         )
 
-    def ext_copy(k, peer):
-        return pltpu.make_async_remote_copy(
-            src_ref=ext_ref.at[peer],
-            dst_ref=re_ref.at[k],
-            send_sem=esend.at[k],
-            recv_sem=erecv.at[k],
-            device_id={"expert": peer},
-            device_id_type=MESH,
-        )
-
-    def issue(k, c):
-        peer = at_partner(k)
-        base_copy(k, peer).start()
-
-        @pl.when(peer < half)
+    def base_copy(k):
+        return side_copy(base_ref, rb_ref, bsend, brecv, k)
+
+    def ext_copy(k):
+        return side_copy(ext_ref, re_ref, esend, erecv, k)
+
+    def pack(b, xs, cots):
+        ids = meta_ref[b, :top, :]
+        share_of = meta_ref[b, top:, :]
+        named = jnp.zeros((8, toks), F32)
+        weight = jnp.zeros((8, toks), F32)
+        for k in range(top):
+            hit = ids[k : k + 1, :] == eight.astype(F32)
+            named += jnp.where(hit, 1.0, 0.0)
+            weight += jnp.where(hit, share_of[k : k + 1, :], 0.0)
+        before = dot(named.astype(BF16), earlier)
+        seen_ref[...] = jnp.where((named > 0.5) & (before < room), before, DROPPED)
+        seen_pw_ref[...] = weight
+        shape = (NX, 16, toks)
+        slot = lax.broadcasted_iota(jnp.int32, shape, 1).astype(F32)
+        ranks = jnp.broadcast_to(seen_ref[:NX, :].reshape(NX, 1, toks), shape)
+        weights = jnp.broadcast_to(seen_pw_ref[:NX, :].reshape(NX, 1, toks), shape)
+        pick = jnp.where((ranks == slot) & (slot < 7.5), 1.0, 0.0).reshape(NX * 16, toks).astype(BF16)
+        scale = jnp.where(ranks == slot - 8.0, weights, 0.0).reshape(NX * 16, toks).astype(BF16)
+        rows = (dot(pick, xs[...]) + dot(scale, cots[...])).reshape(NX, 16, d).astype(BF16)
+        for r in range(NX):
+            base_ref[b * NX + lax.rem(r - zx[1] + NX, NX)] = rows[r]
+
+        @pl.when(low)
         def _():
-            ext_copy(k, peer).start()
-
-        return c
-
-    lax.fori_loop(0, last, issue, 0)
-    rb_ref[last] = base_ref[me]
-
-    @pl.when(low)
-    def _():
-        re_ref[last] = ext_ref[me]
+            shape = (NX, 8, toks)
+            place = lax.broadcasted_iota(jnp.int32, shape, 1)
+            ranks = jnp.broadcast_to(seen_ref[:NX, :].reshape(NX, 1, toks), shape)
+            weights = jnp.broadcast_to(seen_pw_ref[:NX, :].reshape(NX, 1, toks), shape)
+            here = ranks == (8 + place % 2).astype(F32)
+            total = jnp.zeros((NX * 8, wide), F32)
+            for q in range(2):
+                pick = jnp.where(here & (place // 2 == 2 * q), 1.0, 0.0).reshape(NX * 8, toks).astype(BF16)
+                scale = jnp.where(here & (place // 2 == 2 * q + 1), weights, 0.0).reshape(NX * 8, toks).astype(BF16)
+                cols = slice(q * wide, (q + 1) * wide)
+                total += dot(pick, xs[:, cols]) + dot(scale, cots[:, cols])
+            total = total.reshape(NX, 8, wide).astype(BF16)
+            for r in range(NX):
+                ext_ref[b * NX + lax.rem(r - zx[1] + NX, NX)] = total[r]
+            re_ref[b * NX] = ext_ref[b * NX]
+
+        rb_ref[b * NX] = base_ref[b * NX]
+        for j in range(1, NX):
+            base_copy(b * NX + j).start()
+
+            @pl.when(low)
+            def _():
+                ext_copy(b * NX + j).start()
+
+    pack(0, tok_ref, cot_ref)
 
     for load in loads:
         load.wait()
@@ -198,20 +237,23 @@
         )
 
     def v_issue(k, c):
-        v_copy(k).start()
+        @pl.when(k > 0)
+        def _():
+            v_copy(k).start()
+
         return c
 
     def on_group(g, c):
         def arrive(i, c2):
             k = g * many + i
 
-            @pl.when(k < last)
+            @pl.when(lax.rem(k, NX) > 0)
             def _():
-                base_copy(k, me).wait_recv()
-
-            @pl.when((k < last) & low)
+                base_copy(k).wait_recv()
+
+            @pl.when((lax.rem(k, NX) > 0) & low)
             def _():
-                ext_copy(k, 0).wait_recv()
+                ext_copy(k).wait_recv()
 
             return c2
 
@@ -261,7 +303,35 @@
         lax.fori_loop(g * many, g * many + many, v_issue, 0)
         return c
 
-    lax.fori_loop(0, groups - 1, do_group, 0)
+    def on_pair(i, b):
+        meta_copy(b + i).wait_recv()
+        pack(b + i, blk_ref.at[b + i, 0], blk_ref.at[b + i, 1])
+        return b
+
+    def on_step(t, c):
+        for c4 in (0, 3, 1, 2):
+            block_hop(c4, t, tok_ref).wait_recv()
+            if c4 in (0, 3):
+                block_hop(c4, t + 1).start()
+            else:
+
+                @pl.when(t < mid - 1)
+                def _():
+                    block_hop(c4, t + 1).start()
+
+        lax.fori_loop(0, 2, on_pair, 2 * t - 1)
+
+        @pl.when((t > 2) & (lax.rem(t, 2) == 1))
+        def _():
+            do_group((t - 3) // 2, 0)
+
+        return c
+
+    lax.fori_loop(1, mid, on_step, 0)
+    for c in (0, 3):
+        block_hop(c, mid, tok_ref).wait_recv()
+    meta_copy(nz - 1).wait_recv()
+    pack(nz - 1, blk_ref.at[nz - 1, 0], blk_ref.at[nz - 1, 1])
     on_group(groups - 1, 0)
 
     far = ny // 2
@@ -346,8 +416,8 @@
         down = dot(h_ref[...], s_ref[:, at : at + wide], turn)
         ref[...] = down.reshape(ny, 2, few, wide).astype(BF16)
     cross(far, range(4))
-    lax.fori_loop(last - many + 1, last, v_issue, 0)
-    vr_ref[me] = v_ref[last]
+    lax.fori_loop(experts - many, experts, v_issue, 0)
+    vr_ref[me] = v_ref[0]
     t = 0
     for n, off in enumerate(steps[1:]):
         product(off)
@@ -362,7 +432,7 @@
         v_copy(k).wait()
         return c
 
-    lax.fori_loop(0, last, v_finish, 0)
+    lax.fori_loop(1, experts, v_finish, 0)
     values = vr_ref[...].reshape(experts, 128)
     place = rank_ref[...]
     back = jnp.zeros((experts, toks), F32)
@@ -388,15 +458,26 @@
                 hop(i, w, t).wait_send()
 
     def sent(k, c):
-        base_copy(k, me).wait_send()
-
-        @pl.when(at_partner(k) < half)
+        @pl.when(lax.rem(k, NX) > 0)
         def _():
-            ext_copy(k, 0).wait_send()
-
-        return c
-
-    lax.fori_loop(0, last, sent, 0)
+            base_copy(k).wait_send()
+
+        @pl.when((lax.rem(k, NX) > 0) & low)
+        def _():
+            ext_copy(k).wait_send()
+
+        return c
+
+    lax.fori_loop(0, experts, sent, 0)
+
+    def told(n, c):
+        meta_copy(n).wait_send()
+        return c
+
+    lax.fori_loop(1, nz, told, 0)
+    for c in range(4):
+        for t in range(1, mid + (c in (0, 3))):
+            block_hop(c, t, (tok_ref, cot_ref)[c % 2]).wait_send()
 
 
 def pass_kernel(*refs):
@@ -432,9 +513,12 @@
         out_specs=(VMEM,) * 4,
         scratch_shapes=[
             held(experts, toks, dtype=F32),
-            held(experts, toks, dtype=F32),
+            held(8, toks, dtype=F32),
+            held(8, toks, dtype=F32),
+            held(nz, 8, toks, dtype=F32),
+            held(nz, 2, toks, d),
             held(experts, 16, d),
-            held(half, 8, wide),
+            held(experts, 8, wide),
             held(experts, 16, d),
             held(experts, 8, wide),
             held(d, ff),
@@ -453,6 +537,8 @@
         + [held(ny, *s) for s in (gu, gu, dn, dn)] * 2
         + [dma((3,))]
         + [dma((experts,))] * 6
+        + [dma((nz,))] * 2
+        + [dma((4, nz // 2 + 1))] * 2
         + [dma((4, ny))] * 4,
         compiler_params=pltpu.CompilerParams(collective_id=0, has_side_effects=True),
         name="layer",

time: 168 us -> 145 us (0.86)
  the two profiles are of different devices: /device:TPU:2 before, /device:TPU:8 now
where the time goes in v4:
time: 145 us
  Pallas kernels  144 us (99%)
    pallas_call x1, Pallas kernels, per_device(): pl.pallas_call(functools.partial(layer_kernel, nz), out_shape=outs, in_sp...  142 us

profile of v4, /device:TPU:8, one launch (start us, length us, event | category | flops | bytes accessed | tf_op | source)
XLA Modules:
  0.0 144.8 jit_solution(15147340208014359113)
XLA Ops:
  0.6 142.4 %layer.1 = (f32[4,128]{1,0:T(4,128)}, f32[64,384]{1,0:T(8,128)}, f32[64,384]{1,0:T(8,128)}, f32[24,1024]{1,0:T(8,128)}) custom-call(s32[4,128]{1,0:T(4,128)} %bitcast.13, bf16[4,128]{1,0:T(4,128)(2,1)} %bitcast.14, s32[1,32]{1,0:T(1,128)} %bitcast.15, bf16[128,1024]{1,0:T(8,128)(2,1)} %tok_ref.1, bf16[128,1024]{1,0:T(8,128)(2,1)} %cot_ref.1, ...), custom_call_target="tpu_custom_call" | custom-call | tf_op jit(solution)/shard_map/layer/pallas_call | solution.py:509
  143.1 1.7 %hand_on.1 = (f32[4,128]{1,0:T(4,128)}, f32[64,384]{1,0:T(8,128)}, f32[64,384]{1,0:T(8,128)}, f32[24,1024]{1,0:T(8,128)}) custom-call(f32[4,128]{1,0:T(4,128)} %get-tuple-element.12.refs_0_, f32[64,384]{1,0:T(8,128)} %get-tuple-element.13.refs_1_, f32[64,384]{1,0:T(8,128)} %get-tuple-element.14.refs_2_, f32[24,1024]{1,0:T(8,128)} %get-tuple-element.15.refs_3_), custom_call_target="tpu_custom_call" | custom-call | tf_op jit(solution)/shard_map/hand_on/pallas_call | solution.py:546
